TPU v7x, 128 devices: a whole 4x4x4 slice. The times are simulated.
128 devices in a mesh: ice: 8 (over x, core), ocn: 16 (over z, y).
Axes of the slice: x: 4, y: 4, z: 4, core: 2. Of those that a mesh axis runs over, the one named last changes fastest.
Arguments:
- ice_state: bfloat16 [5, 20, 131072], P(None, None, ('ice', 'ocn')), may hold values from -6 to 6
- ocean_state: bfloat16 [5, 20, 131072], P(None, None, ('ice', 'ocn')), may hold values from -5 to 5
- ice_rate: float32 [5, 20], replicated, may hold values from 0.2 to 2
- block_weights: bfloat16 [16384, 128, 128], P(('ice', 'ocn')), may hold values from -0.1875 to 0.1875
- block_route: int32 [16384, 1], P(('ice', 'ocn')), may hold values from 0 to 127; in each aligned block of 128 rows (0 to 127, 128 to 255, ...) at most 2 rows name the same one
- block_tiles: int32 [16384, 2], P(('ice', 'ocn')), may hold values from 0 to 7
- block_valid: int32 [16384], P(('ice', 'ocn')), may hold values from 16 to 128
- ice_mask: int32 [131072], P(('ice', 'ocn')), may hold values 0 or 1
Outputs:
- ice_final: bfloat16 [5, 20, 131072], P(None, None, ('ice', 'ocn'))
- ocean_flux: bfloat16 [5, 20, 131072], P(None, None, ('ice', 'ocn'))
Inputs may be any that keep to these rules, and one draw needn't show every extreme that they name: `block_route`: among the blocks of one device no destination appears more than 2 times.
All inputs are finite; a program needn't handle non-finite values. No bound on the sum of `ice_mask` on one device may be relied on, other than what follows from the above.
Results may differ from a plain program's by a relative error of at most 0.008.
Values may be sent and summed in bfloat16 or wider, within the bound.
No kernel may reach another device: no remote copies, remote signals or barrier semaphores. Data moves between devices by JAX's collectives and lax.ppermute only.
A program may use at most 128 MiB of HBM per device.

v0:
```python
import jax
import jax.numpy as jnp
from jax import lax
from jax.experimental import pallas as pl
from jax.experimental.pallas import tpu as pltpu
from jax.sharding import PartitionSpec as P


AXES = ("ice", "ocn")
BF = jnp.bfloat16
F32 = jnp.float32
ROWS = 104
UNIT = 16
SENT = 124
LATE = 148
SPARE = 8
LATE_SPAN = 9600
HALVES = 2
DIMS = {"x1": (0, 1), "x3": (0, 3), "c": (1, 1), "z1": (2, 1), "z3": (2, 3), "y1": (3, 1), "y3": (3, 3)}
OCN_DIMS = ("z1", "y1", "z3", "y3")
ICE_DIMS = ("x1", "x3")
COLOURS = 4
PER = 8 // COLOURS
BITS1 = (0, 1, 1, 0)
BITS3 = (0, 0, 1, 1)


def ocn_dim(colour, step):
    return OCN_DIMS[(colour + step) % 4]


def ice_dim(core, step):
    return ICE_DIMS[(core + step) % 2]


def swap(value, names):
    pairs = []
    for x in range(4):
        for c in range(2):
            for z in range(4):
                for y in range(4):
                    here = [x, c, z, y]
                    there = list(here)
                    axis, flip = DIMS[names[c]]
                    there[axis] ^= flip
                    pairs.append(tuple((q[0] * 2 + q[1]) * 16 + q[2] * 4 + q[3] for q in (here, there)))
    return lax.ppermute(value, AXES, pairs)


def swap_ocn(value, colour, step):
    return swap(value, [ocn_dim(colour, step)] * 2)


def swap_ice(value, step):
    return swap(value, [ice_dim(core, step) for core in range(2)])


def swap_core(value):
    return swap(value, ["c", "c"])


def pack_kernel(base_ref, valid_ref, w_ref, rows_ref):
    step = pl.program_id(0)
    per = w_ref.shape[0]
    rows = lax.broadcasted_iota(jnp.int32, (UNIT, 128), 0)

    def body(n, carry):
        block = step * per + n
        base = base_ref[block]
        valid = valid_ref[block]

        @pl.when(base >= 0)
        def _():
            rows_ref[pl.ds(base, 8)] = w_ref[n].reshape(8, UNIT, 128)
            last = lax.shift_right_logical(valid - 1, 4)
            unit = w_ref[n, pl.ds(pl.multiple_of(last * UNIT, UNIT), UNIT), :]
            rows_ref[base + last] = jnp.where(rows < valid - last * UNIT, unit.astype(F32), 0.0).astype(BF)

        return carry

    lax.fori_loop(0, per, body, 0)


def pack(sent, base, valid, weights):
    steps = 8
    per = weights.shape[0] // steps
    width = sent + SPARE
    rows = pl.pallas_call(
        pack_kernel,
        grid_spec=pltpu.PrefetchScalarGridSpec(
            num_scalar_prefetch=2,
            grid=(steps,),
            in_specs=[pl.BlockSpec((per, 128, 128), lambda g, *_: (g, 0, 0))],
            out_specs=pl.BlockSpec(memory_space=pltpu.VMEM),
        ),
        out_shape=jax.ShapeDtypeStruct((8 * width, UNIT, 128), BF),
        compiler_params=pltpu.CompilerParams(vmem_limit_bytes=12 << 20),
        name="pack_rows",
    )(base, valid, weights)
    return rows.reshape(8, width, UNIT, 128)[:, :sent]


def block_rows(w_ref, start, count):
    parts = []
    last = w_ref.shape[0] - 1
    for r in range(8):
        unit = w_ref[jnp.minimum(start + r, last)]
        parts.append(jnp.where(r < count, unit, jnp.zeros_like(unit)))
    return jnp.concatenate(parts, axis=0)


GROUP = 8
LISTED = 272
TABLES = 2
VMEM_SPEC = pl.BlockSpec(memory_space=pltpu.VMEM)
SMEM_SPEC = pl.BlockSpec(memory_space=pltpu.SMEM)
HBM_SPEC = pl.BlockSpec(memory_space=pltpu.HBM)
HALF = 64
STAGES = [
    pltpu.VMEM((8 * SENT, UNIT, 128), BF),
    pltpu.VMEM((8, UNIT, 128), BF),
    pltpu.SemaphoreType.DMA((9,)),
]


def fetch(counts_ref, moved_ref, stages, turn):
    span = pl.ds(counts_ref[3 + turn] * SENT, SENT)
    return pltpu.make_async_copy(moved_ref.at[span], stages[0].at[span], stages[2].at[turn])


def start_fetch(counts_ref, moved_ref, stages):
    def start(turn, carry):
        fetch(counts_ref, moved_ref, stages, turn).start()
        return carry

    lax.fori_loop(0, 8, start, 0)


def each_tile(count, action):
    def step(i, carry):
        action(i)
        return carry

    lax.fori_loop(0, count, step, 0, unroll=4)


def clear(ref):
    def action(i):
        ref[i] = jnp.zeros(ref.shape[1:], ref.dtype)

    each_tile(ref.shape[0], action)


def copy_tiles(source, low, target, base, count):
    def action(i):
        target[base + i] = source[low + i].astype(target.dtype)

    each_tile(count, action)


def add_blocks(list_ref, counts_ref, moved_ref, late_ref, stages, left, acc, forwards):
    rows_ref, late, sem = stages

    def product(word, w_ref, start):
        w = block_rows(w_ref, start, lax.shift_right_logical(word, 11) & 15)
        tile = left[lax.shift_right_logical(word, 15 if forwards else 21) & 63]
        contract = 0 if forwards else 1
        return lax.dot_general(tile, w, (((1,), (contract,)), ((), ())), preferred_element_type=F32)

    def add(word, value):
        at = lax.shift_right_logical(word, 21 if forwards else 15) & 63
        acc[at] = acc[at] + value

    def wait(source, carry):
        fetch(counts_ref, moved_ref, stages, source).wait()
        return carry

    def body(i, waited):
        words = [list_ref[i * GROUP + u] for u in range(GROUP)]
        needed = waited
        for word in words:
            needed = jnp.maximum(needed, lax.shift_right_logical(word, 27) + 1)
        lax.fori_loop(waited, needed, wait, 0)
        prods = [product(word, rows_ref, word & 2047) for word in words]
        for word, value in zip(words, prods):
            add(word, value)
        return needed

    waited = lax.fori_loop(0, counts_ref[0], body, 0)
    lax.fori_loop(waited, 8, wait, 0)

    def late_body(j, carry):
        word = list_ref[j]
        copy = pltpu.make_async_copy(late_ref.at[pl.ds(word & 2047, 8)], late, sem.at[8])
        copy.start()
        copy.wait()
        add(word, product(word, late, 0))
        return carry

    lax.fori_loop(counts_ref[1], counts_ref[2], late_body, 0)


def forward_kernel(list_ref, counts_ref, *rest):
    ice_ref, moved_ref, late_ref, send0, send1, keep0, keep1, acc, *stages = rest
    start_fetch(counts_ref, moved_ref, stages)
    clear(acc)
    add_blocks(list_ref, counts_ref, moved_ref, late_ref, stages, ice_ref, acc, True)
    for i, (send, keep) in enumerate(((send0, keep0), (send1, keep1))):
        copy_tiles(acc, i * 32, keep, 0, 16)
        copy_tiles(acc, i * 32 + 16, send, 0, 16)


def forward(tables, ice_all, moved, late):
    outs = pl.pallas_call(
        forward_kernel,
        in_specs=[SMEM_SPEC] * TABLES + [VMEM_SPEC] + [HBM_SPEC] * 2,
        out_specs=[VMEM_SPEC] * 4,
        out_shape=[jax.ShapeDtypeStruct((16, ROWS, 128), BF)] * 2 + [jax.ShapeDtypeStruct((16, ROWS, 128), F32)] * 2,
        scratch_shapes=[pltpu.VMEM((HALF, ROWS, 128), F32)] + STAGES,
        compiler_params=pltpu.CompilerParams(vmem_limit_bytes=16 << 20),
        name="products",
    )(*tables, ice_all, moved, late)
    return outs[:2], outs[2:]


def first_backward_kernel(list_ref, counts_ref, *rest):
    pieces, (moved_ref, late_ref, acc, flux, *stages) = rest[:4], rest[4:]
    start_fetch(counts_ref, moved_ref, stages)
    for i, piece in enumerate(pieces):
        copy_tiles(piece, 0, flux, i * 16, 16)
    clear(acc)
    add_blocks(list_ref, counts_ref, moved_ref, late_ref, stages, flux, acc, False)


def first_backward(tables, pieces, moved, late):
    return pl.pallas_call(
        first_backward_kernel,
        in_specs=[SMEM_SPEC] * TABLES + [VMEM_SPEC] * 4 + [HBM_SPEC] * 2,
        out_specs=VMEM_SPEC,
        out_shape=jax.ShapeDtypeStruct((64, ROWS, 128), F32),
        scratch_shapes=[pltpu.VMEM((HALF, ROWS, 128), BF)] + STAGES,
        compiler_params=pltpu.CompilerParams(vmem_limit_bytes=16 << 20),
        name="returns",
    )(*tables, *pieces, moved, late)


def last_backward_kernel(list_ref, counts_ref, *rest):
    pieces, (so_far, moved_ref, late_ref, send, keep, flux, acc, *stages) = rest[:4], rest[4:]
    start_fetch(counts_ref, moved_ref, stages)
    for i, piece in enumerate(pieces):
        copy_tiles(piece, 0, flux, i * 16, 16)
    copy_tiles(so_far, 0, acc, 0, 64)
    add_blocks(list_ref, counts_ref, moved_ref, late_ref, stages, flux, acc, False)
    copy_tiles(acc, 0, keep, 0, 32)
    copy_tiles(acc, 32, send, 0, 32)


def last_backward(tables, pieces, so_far, moved, late):
    return pl.pallas_call(
        last_backward_kernel,
        in_specs=[SMEM_SPEC] * TABLES + [VMEM_SPEC] * 5 + [HBM_SPEC] * 2,
        out_specs=[VMEM_SPEC] * 2,
        out_shape=[jax.ShapeDtypeStruct((32, ROWS, 128), BF), jax.ShapeDtypeStruct((32, ROWS, 128), F32)],
        scratch_shapes=[pltpu.VMEM((HALF, ROWS, 128), BF), pltpu.VMEM((64, ROWS, 128), F32)] + STAGES,
        compiler_params=pltpu.CompilerParams(vmem_limit_bytes=16 << 20),
        name="returns",
    )(*tables, *pieces, so_far, moved, late)


def nothing():
    return pl.pallas_call(
        lambda out_ref: None,
        out_specs=HBM_SPEC,
        out_shape=jax.ShapeDtypeStruct((LATE_SPAN, UNIT, 128), BF),
        name="unread",
    )()


def gather_ice_step(own, step):
    return jnp.concatenate([own, swap_ice(own, step)], 0)


def gather_ice_cores(line):
    return jnp.concatenate([line, swap_core(line)], 0)


def scatter_ice(send, keep):
    part = keep + swap_core(send).astype(F32)
    for step in (1, 0):
        n = part.shape[0] // 2
        part = part[:n] + swap_ice(part[n:].astype(BF), step).astype(F32)
    return part


def scatter_ocn(send, keep, colour):
    got = swap_ocn(send, colour, 0)
    for step in range(1, 4):
        n = keep.shape[0] // 2
        send = (keep[n:] + got[n:].astype(F32)).astype(BF)
        keep = keep[:n] + got[:n].astype(F32)
        got = swap_ocn(send, colour, step)
    return keep + got.astype(F32)


def gather_ocn(own, colour):
    for step in (3, 2, 1):
        own = jnp.concatenate([own, swap_ocn(own, colour, step)], 0)
    return [own, swap_ocn(own, colour, 0)]


def bit_of(displacement, name):
    bits = BITS1 if name.endswith("1") else BITS3
    value = jnp.zeros_like(displacement)
    for d in range(4):
        if bits[d]:
            value = value | (displacement == d).astype(jnp.int32)
    return value


def move(packed):
    sent = packed.shape[1]
    packed = packed.reshape(8, sent * UNIT, 128)
    moved = lax.all_to_all(packed, "ice", split_axis=0, concat_axis=0, tiled=True)
    return moved.reshape(8 * sent, UNIT, 128)


def on_device(ice_state, ocean_state, ice_rate, block_weights, block_route, block_tiles, block_valid, ice_mask):
    cats, fields, cells = ice_state.shape
    chans = cats * fields
    pad = ROWS - chans
    blocks = block_weights.shape[0]
    row, col = lax.axis_index("ice"), lax.axis_index("ocn")

    def tiled(value):
        value = value.reshape(chans, 8, 128).transpose(1, 0, 2)
        return jnp.pad(value, ((0, 0), (0, pad), (0, 0)))

    def untiled(value):
        return value[:, :chans].transpose(1, 0, 2).reshape(cats, fields, cells)

    route = block_route[:, 0]
    bucket = route >> 4
    units = (block_valid + UNIT - 1) // UNIT
    order = jnp.arange(blocks, dtype=jnp.int32)
    earlier = (bucket[None, :] == bucket[:, None]) & (order[None, :] < order[:, None])
    offset = jnp.sum(jnp.where(earlier, units[None, :], 0), axis=1)
    fit = offset + units <= SENT
    late_offset = jnp.sum(jnp.where(earlier & ~fit[None, :], units[None, :], 0), axis=1)
    base = jnp.where(fit, bucket * (SENT + SPARE) + offset, -1)
    late_base = jnp.where(fit, -1, bucket * (LATE + SPARE) + late_offset)
    facts = jnp.stack(
        [
            units + 16 * jnp.max((~fit).astype(jnp.int32)),
            block_tiles[:, 0] * 8 + block_tiles[:, 1],
            route + jnp.where(fit, 0, 128),
            jnp.where(fit, offset, late_offset),
        ]
    ).astype(BF)

    land = ice_mask.astype(F32).reshape(8, 1, 128)
    rates = jnp.pad(ice_rate.reshape(chans, 1), ((0, pad), (0, 0)))[None]
    ice = tiled(ice_state) * land.astype(BF)
    ice = ice + jnp.pad(facts[None], ((0, 7), (chans, 0), (0, 0)))
    packed = pack(SENT, base, block_valid, block_weights)
    line = gather_ice_step(ice, 0)
    packed, line = lax.optimization_barrier((packed, line))
    moved = move(packed)
    got = swap_ice(line, 1)
    line = jnp.concatenate([line, got], 0)
    got = swap_core(line)
    ice_all = jnp.concatenate([line, got], 0)

    table = jnp.stack([ice_all[8 * place, chans:] for place in range(8)]).astype(jnp.int32)
    units, code, route, offset = (table[:, f] for f in range(4))
    group_late = jnp.max(units[:, 0]) >= 16
    units = units & 15
    fit = route < 128
    mine = ((route >> 4) & 7) == row
    column = route & 15
    ice_tile, ocean_tile = code >> 3, code & 7
    places = jnp.arange(8, dtype=jnp.int32)[:, None]
    core = row & 1
    from_core = (places >> 2) ^ core
    high, low = (places >> 1) & 1, places & 1
    bit1 = jnp.where(from_core == 0, low, high)
    bit3 = jnp.where(from_core == 0, high, low)
    sources = (((bit1 ^ (bit3 * 3)) ^ (row >> 1)) << 1) | from_core
    start = sources * jnp.where(fit, SENT, LATE) + offset
    ice_at = places * 8 + ice_tile
    dz = (column >> 2) ^ (col >> 2)
    dy = (column & 3) ^ (col & 3)
    bits = {name: bit_of(dz if name[0] == "z" else dy, name) for name in OCN_DIMS}
    colour = ocean_tile // PER
    place = jnp.zeros_like(colour)
    for k in range(COLOURS):
        inner = jnp.zeros_like(colour)
        for step in range(4):
            inner = inner * 2 + bits[ocn_dim(k, step)]
        place = jnp.where(colour == k, inner, place)
    out_at = (colour & 1) * 32 + place * PER + ocean_tile % PER
    word = start | (units << 11) | (ice_at << 15) | (out_at << 21) | (places << 27)
    ahead = order[None, :] < order[:, None]
    sooner = places.T < places
    tables = []
    for h in range(HALVES):
        chosen = mine & ((ocean_tile >> 2) == h)
        here, later = chosen & fit, chosen & ~fit
        spots = []
        for some in (here, later):
            count = jnp.sum(some.astype(jnp.int32), axis=1)
            before = jnp.sum(jnp.where(sooner, count[None, :], 0), axis=1)
            rank = jnp.sum((some[:, None, :] & ahead[None]).astype(jnp.int32), axis=2)
            spots.append((before[:, None] + rank, jnp.sum(count)))
        groups = (spots[0][1] + GROUP - 1) // GROUP
        at = jnp.where(here, spots[0][0], jnp.where(later, groups * GROUP + spots[1][0], -1))
        listed = jnp.where(at[..., None] == jnp.arange(LISTED, dtype=jnp.int32), word[..., None], 0)
        counts = jnp.stack([groups, groups * GROUP, groups * GROUP + spots[1][1]])
        tables.append([jnp.sum(listed, axis=(0, 1)), jnp.concatenate([counts, sources[:, 0]])])
    moved, group_late = lax.optimization_barrier((moved, group_late))
    late = lax.cond(
        group_late,
        lambda: jnp.pad(
            move(pack(LATE, late_base, block_valid, block_weights)),
            ((0, LATE_SPAN - 8 * LATE), (0, 0), (0, 0)),
        ),
        nothing,
    )

    ocean = tiled(ocean_state)
    flux = None
    for turn in range(2):
        if turn:
            ice_all = gather_ice_cores(gather_ice_step(gather_ice_step(ice, 0), 1))
        flux = []
        for h in range(HALVES):
            sends, keeps = forward(tables[h], ice_all, moved, late)
            for i in range(2):
                k = 2 * h + i
                total = scatter_ocn(sends[i], keeps[i], k)
                flux.append(jnp.tanh(total + ocean[PER * k : PER * (k + 1)].astype(F32)).astype(BF))
        pieces = [gather_ocn(flux[k], k) for k in range(COLOURS)]
        so_far = first_backward(tables[0], pieces[0] + pieces[1], moved, late)
        send, keep = last_backward(tables[1], pieces[2] + pieces[3], so_far, moved, late)
        forcing = scatter_ice(send, keep)
        ice = (land * (ice.astype(F32) + rates * jnp.tanh(forcing))).astype(BF)
    return untiled(ice), untiled(jnp.concatenate(flux, 0))


def solution(mesh):
    placed = (
        P(None, None, AXES),
        P(None, None, AXES),
        P(),
        P(AXES, None, None),
        P(AXES, None),
        P(AXES, None),
        P(AXES),
        P(AXES),
    )
    return jax.shard_map(
        on_device,
        mesh=mesh,
        in_specs=placed,
        out_specs=(P(None, None, AXES), P(None, None, AXES)),
        check_vma=False,
    )
```

profile of v0, /device:TPU:0, one launch (start us, length us, event | category | flops | bytes accessed | tf_op | source)
XLA Modules:
  0.0 315.8 jit_solution(7562123554794084658)
XLA Ops:
  8.6 6.4 %pack_rows.3 = bf16[1056,16,128]{2,1,0:T(8,128)(2,1)S(1)} custom-call(s32[128]{0:T(128)S(1)} %get-tuple-element.157.base_ref, s32[128]{0:T(128)} %valid_ref.1, bf16[128,128,128]{2,1,0:T(8,128)(2,1)} %w_ref.1), custom_call_target="tpu_custom_call" | custom-call | tf_op jit(solution)/shard_map/pack_rows/pallas_call | solution.py:88
  15.0 2.6 slice.516
  19.9 7.2 %collective-permute-done.1 = bf16[16,104,128]{2,1,0:T(8,128)(2,1)S(1)} collective-permute-done((bf16[16,104,128]{2,1,0:T(8,128)(2,1)S(1)}, bf16[16,104,128]{2,1,0:T(8,128)(2,1)S(1)}, u32[]{:S(2)}, u32[]{:S(2)}) %collective-permute-start.1) | collective-permute-done | bytes 426016 | tf_op jit(solution)/shard_map/ppermute | solution.py:47
  28.1 4.6 %all-to-all-start.1 = ((bf16[8,1984,128]{2,1,0:T(8,128)(2,1)}), bf16[8,1984,128]{2,1,0:T(8,128)(2,1)}, u32[]{:S(2)}, u32[]{:S(2)}) async-start(bf16[8,1984,128]{2,1,0:T(8,128)(2,1)} %bitcast.231), calls=%async_computation.1 | async-start | bytes 8126464 | tf_op jit(solution)/shard_map/all_to_all | solution.py:323
  43.4 37.5 %all-to-all-done.1 = bf16[8,1984,128]{2,1,0:T(8,128)(2,1)} async-done(((bf16[8,1984,128]{2,1,0:T(8,128)(2,1)}), bf16[8,1984,128]{2,1,0:T(8,128)(2,1)}, u32[]{:S(2)}, u32[]{:S(2)}) %all-to-all-start.1) | async-done | bytes 4063264 | tf_op jit(solution)/shard_map/all_to_all | solution.py:323
  80.9 5.9 %products.5 = (bf16[16,104,128]{2,1,0:T(8,128)(2,1)S(1)}, bf16[16,104,128]{2,1,0:T(8,128)(2,1)S(1)}, f32[16,104,128]{2,1,0:T(8,128)S(1)}, f32[16,104,128]{2,1,0:T(8,128)S(1)}) custom-call(s32[272]{0:T(512)S(1)} %get-tuple-element.79.list_ref, s32[11]{0:T(128)S(1)} %get-tuple-element.159.counts_ref, ...), custom_call_target="tpu_custom_call" | custom-call | tf_op jit(solution)/shard_map/products/pallas_call | solution.py:214
  88.1 4.6 %products.4 = (bf16[16,104,128]{2,1,0:T(8,128)(2,1)S(1)}, bf16[16,104,128]{2,1,0:T(8,128)(2,1)S(1)}, f32[16,104,128]{2,1,0:T(8,128)S(1)}, f32[16,104,128]{2,1,0:T(8,128)S(1)}) custom-call(s32[272]{0:T(512)S(1)} %get-tuple-element.80.list_ref, s32[11]{0:T(128)S(1)} %get-tuple-element.160.counts_ref, ...), custom_call_target="tpu_custom_call" | custom-call | tf_op jit(solution)/shard_map/products/pallas_call | solution.py:214
  92.7 3.0 collective-permute-start.11
  101.8 3.2 %collective-permute-done.11 = bf16[16,104,128]{2,1,0:T(8,128)(2,1)S(1)} collective-permute-done((bf16[16,104,128]{2,1,0:T(8,128)(2,1)S(1)}, bf16[16,104,128]{2,1,0:T(8,128)(2,1)S(1)}, u32[]{:S(2)}, u32[]{:S(2)}) %collective-permute-start.11) | collective-permute-done | bytes 426016 | tf_op jit(solution)/shard_map/ppermute | solution.py:47
  107.5 2.9 collective-permute-done.3
  114.7 2.5 collective-permute-start.21
  119.9 3.0 collective-permute-start.14
  125.3 3.0 collective-permute-done.22
  154.6 5.0 %collective-permute-done.26.rest_1_ = bf16[16,104,128]{2,1,0:T(8,128)(2,1)S(1)} collective-permute-done((bf16[16,104,128]{2,1,0:T(8,128)(2,1)S(1)}, bf16[16,104,128]{2,1,0:T(8,128)(2,1)S(1)}, u32[]{:S(2)}, u32[]{:S(2)}) %collective-permute-start.26) | collective-permute-done | bytes 426016 | tf_op jit(solution)/shard_map/ppermute | solution.py:47
  160.4 5.8 %returns.4.rest_4_ = f32[64,104,128]{2,1,0:T(8,128)S(1)} custom-call(s32[272]{0:T(512)S(1)} %get-tuple-element.79.list_ref, s32[11]{0:T(128)S(1)} %get-tuple-element.159.counts_ref, bf16[16,104,128]{2,1,0:T(8,128)(2,1)S(1)} %pad_maximum_fusion.6.rest_0_, bf16[16,104,128]{2,1,0:T(8,128)(2,1)S(1)} %collective-permute-done.26.rest_1_, ...), custom_call_target="tpu_custom_call" | custom-call | tf_op jit(solution)/shard_map/returns/pallas_call | solution.py:236
  166.2 4.7 %returns.5 = (bf16[32,104,128]{2,1,0:T(8,128)(2,1)S(1)}, f32[32,104,128]{2,1,0:T(8,128)S(1)}) custom-call(s32[272]{0:T(512)S(1)} %get-tuple-element.80.list_ref, s32[11]{0:T(128)S(1)} %get-tuple-element.160.counts_ref, bf16[16,104,128]{2,1,0:T(8,128)(2,1)S(1)} %pad_maximum_fusion.4.rest_0_, bf16[16,104,128]{2,1,0:T(8,128)(2,1)S(1)} %collective-permute-done.10.rest_1_, ...), custom_call_target="tpu_custom_call" | custom-call | tf_op jit(solution)/shard_map/returns/pallas_call | solution.py:259
  171.0 2.4 collective-permute-done.35
  174.8 8.2 %collective-permute-done.36 = bf16[16,104,128]{2,1,0:T(8,128)(2,1)S(1)} collective-permute-done((bf16[16,104,128]{2,1,0:T(8,128)(2,1)S(1)}, bf16[16,104,128]{2,1,0:T(8,128)(2,1)S(1)}, u32[]{:S(2)}, u32[]{:S(2)}) %collective-permute-start.36) | collective-permute-done | bytes 426016 | tf_op jit(solution)/shard_map/ppermute | solution.py:47
  183.3 5.7 %collective-permute-done.37 = bf16[8,104,128]{2,1,0:T(8,128)(2,1)S(1)} collective-permute-done((bf16[8,104,128]{2,1,0:T(8,128)(2,1)S(1)}, bf16[8,104,128]{2,1,0:T(8,128)(2,1)S(1)}, u32[]{:S(2)}, u32[]{:S(2)}) %collective-permute-start.37) | collective-permute-done | bytes 213024 | tf_op jit(solution)/shard_map/ppermute | solution.py:47
  189.3 5.8 %collective-permute-done.38 = bf16[8,104,128]{2,1,0:T(8,128)(2,1)S(1)} collective-permute-done((bf16[8,104,128]{2,1,0:T(8,128)(2,1)S(1)}, bf16[8,104,128]{2,1,0:T(8,128)(2,1)S(1)}, u32[]{:S(2)}, u32[]{:S(2)}) %collective-permute-start.38) | collective-permute-done | bytes 213024 | tf_op jit(solution)/shard_map/ppermute | solution.py:47
  196.3 8.2 %collective-permute-done.39 = bf16[16,104,128]{2,1,0:T(8,128)(2,1)S(1)} collective-permute-done((bf16[16,104,128]{2,1,0:T(8,128)(2,1)S(1)}, bf16[16,104,128]{2,1,0:T(8,128)(2,1)S(1)}, u32[]{:S(2)}, u32[]{:S(2)}) %collective-permute-start.39) | collective-permute-done | bytes 426016 | tf_op jit(solution)/shard_map/ppermute | solution.py:47
  207.3 5.9 %products.7 = (bf16[16,104,128]{2,1,0:T(8,128)(2,1)S(1)}, bf16[16,104,128]{2,1,0:T(8,128)(2,1)S(1)}, f32[16,104,128]{2,1,0:T(8,128)S(1)}, f32[16,104,128]{2,1,0:T(8,128)S(1)}) custom-call(s32[272]{0:T(512)S(1)} %get-tuple-element.79.list_ref, s32[11]{0:T(128)S(1)} %get-tuple-element.159.counts_ref, bf16[64,104,128]{2,1,0:T(8,128)(2,1)S(1)} %pad_maximum_fusion.rest_0_, ...), custom_call_target="tpu_custom_call" | custom-call | tf_op jit(solution)/shard_map/products/pallas_call | solution.py:214
  214.9 4.6 %products.6 = (bf16[16,104,128]{2,1,0:T(8,128)(2,1)S(1)}, bf16[16,104,128]{2,1,0:T(8,128)(2,1)S(1)}, f32[16,104,128]{2,1,0:T(8,128)S(1)}, f32[16,104,128]{2,1,0:T(8,128)S(1)}) custom-call(s32[272]{0:T(512)S(1)} %get-tuple-element.80.list_ref, s32[11]{0:T(128)S(1)} %get-tuple-element.160.counts_ref, bf16[64,104,128]{2,1,0:T(8,128)(2,1)S(1)} %pad_maximum_fusion.rest_0_, ...), custom_call_target="tpu_custom_call" | custom-call | tf_op jit(solution)/shard_map/products/pallas_call | solution.py:214
  219.5 2.7 collective-permute-start.49
  226.9 5.6 %collective-permute-done.49 = bf16[16,104,128]{2,1,0:T(8,128)(2,1)S(1)} collective-permute-done((bf16[16,104,128]{2,1,0:T(8,128)(2,1)S(1)}, bf16[16,104,128]{2,1,0:T(8,128)(2,1)S(1)}, u32[]{:S(2)}, u32[]{:S(2)}) %collective-permute-start.49) | collective-permute-done | bytes 426016 | tf_op jit(solution)/shard_map/ppermute | solution.py:47
  247.7 2.4 collective-permute-start.52
  274.4 3.3 %collective-permute-done.63 = bf16[8,104,128]{2,1,0:T(8,128)(2,1)S(1)} collective-permute-done((bf16[8,104,128]{2,1,0:T(8,128)(2,1)S(1)}, bf16[8,104,128]{2,1,0:T(8,128)(2,1)S(1)}, u32[]{:S(2)}, u32[]{:S(2)}) %collective-permute-start.63) | collective-permute-done | bytes 213024 | tf_op jit(solution)/shard_map/ppermute | solution.py:47
  280.4 5.5 %collective-permute-done.64.rest_1_ = bf16[16,104,128]{2,1,0:T(8,128)(2,1)S(1)} collective-permute-done((bf16[16,104,128]{2,1,0:T(8,128)(2,1)S(1)}, bf16[16,104,128]{2,1,0:T(8,128)(2,1)S(1)}, u32[]{:S(2)}, u32[]{:S(2)}) %collective-permute-start.64) | collective-permute-done | bytes 426016 | tf_op jit(solution)/shard_map/ppermute | solution.py:47
  286.1 5.8 %returns.6.rest_4_ = f32[64,104,128]{2,1,0:T(8,128)S(1)} custom-call(s32[272]{0:T(512)S(1)} %get-tuple-element.79.list_ref, s32[11]{0:T(128)S(1)} %get-tuple-element.159.counts_ref, bf16[16,104,128]{2,1,0:T(8,128)(2,1)S(1)} %pad_maximum_fusion.11.rest_0_, bf16[16,104,128]{2,1,0:T(8,128)(2,1)S(1)} %collective-permute-done.64.rest_1_, ...), custom_call_target="tpu_custom_call" | custom-call | tf_op jit(solution)/shard_map/returns/pallas_call | solution.py:236
  291.9 4.7 %returns.7 = (bf16[32,104,128]{2,1,0:T(8,128)(2,1)S(1)}, f32[32,104,128]{2,1,0:T(8,128)S(1)}) custom-call(s32[272]{0:T(512)S(1)} %get-tuple-element.80.list_ref, s32[11]{0:T(128)S(1)} %get-tuple-element.160.counts_ref, bf16[16,104,128]{2,1,0:T(8,128)(2,1)S(1)} %pad_maximum_fusion.9.rest_0_, bf16[16,104,128]{2,1,0:T(8,128)(2,1)S(1)} %collective-permute-done.48.rest_1_, ...), custom_call_target="tpu_custom_call" | custom-call | tf_op jit(solution)/shard_map/returns/pallas_call | solution.py:259
  299.9 8.8 %collective-permute-done.74 = bf16[16,104,128]{2,1,0:T(8,128)(2,1)S(1)} collective-permute-done((bf16[16,104,128]{2,1,0:T(8,128)(2,1)S(1)}, bf16[16,104,128]{2,1,0:T(8,128)(2,1)S(1)}, u32[]{:S(2)}, u32[]{:S(2)}) %collective-permute-start.74) | collective-permute-done | bytes 426016 | tf_op jit(solution)/shard_map/ppermute | solution.py:47
  309.8 4.9 %collective-permute-done.75 = bf16[8,104,128]{2,1,0:T(8,128)(2,1)S(1)} collective-permute-done((bf16[8,104,128]{2,1,0:T(8,128)(2,1)S(1)}, bf16[8,104,128]{2,1,0:T(8,128)(2,1)S(1)}, u32[]{:S(2)}, u32[]{:S(2)}) %collective-permute-start.75) | collective-permute-done | bytes 213024 | tf_op jit(solution)/shard_map/ppermute | solution.py:47
  (258 shorter events, 124.0 us)
Async XLA Ops:
  6.9 10.7 %collective-permute-start = (bf16[8,104,128]{2,1,0:T(8,128)(2,1)S(1)}, bf16[8,104,128]{2,1,0:T(8,128)(2,1)S(1)}, u32[]{:S(2)}, u32[]{:S(2)}) collective-permute-start(bf16[8,104,128]{2,1,0:T(8,128)(2,1)S(1)} %fusion.19), channel_id=1, source_target_pairs={{0,32},{1,33},{2,34},{3,35},{4,36},{5,37},{6,38},{7,39},{8,40},{9,... | collective-permute-start | bytes 638984 | tf_op jit(solution)/shard_map/ppermute | solution.py:47
  17.7 9.4 %collective-permute-start.1 = (bf16[16,104,128]{2,1,0:T(8,128)(2,1)S(1)}, bf16[16,104,128]{2,1,0:T(8,128)(2,1)S(1)}, u32[]{:S(2)}, u32[]{:S(2)}) collective-permute-start(bf16[16,104,128]{2,1,0:T(8,128)(2,1)S(1)} %pad_maximum_fusion.3), channel_id=1, source_target_pairs={{0,96},{1,97},{2,98},{3,99},{4,100},{5,101},{6,102},{7,103},{8,104... | collective-permute-start | bytes 1277960 | tf_op jit(solution)/shard_map/ppermute | solution.py:47
  28.1 52.8 %all-to-all-start.1 = ((bf16[8,1984,128]{2,1,0:T(8,128)(2,1)}), bf16[8,1984,128]{2,1,0:T(8,128)(2,1)}, u32[]{:S(2)}, u32[]{:S(2)}) async-start(bf16[8,1984,128]{2,1,0:T(8,128)(2,1)} %bitcast.231), calls=%async_computation.1 | async-start | bytes 8126464 | tf_op jit(solution)/shard_map/all_to_all | solution.py:323
  86.8 13.3 %collective-permute-start.27 = (bf16[16,104,128]{2,1,0:T(8,128)(2,1)S(1)}, bf16[16,104,128]{2,1,0:T(8,128)(2,1)S(1)}, u32[]{:S(2)}, u32[]{:S(2)}) collective-permute-start(bf16[16,104,128]{2,1,0:T(8,128)(2,1)S(1)} %get-tuple-element.62), channel_id=1, source_target_pairs={{0,1},{1,0},{2,3},{3,2},{4,5},{5,4},{6,7},{7,6},{8,9},{9,8},{10,11... | collective-permute-start | bytes 1277960 | tf_op jit(solution)/shard_map/ppermute | solution.py:47
  92.7 12.3 %collective-permute-start.11 = (bf16[16,104,128]{2,1,0:T(8,128)(2,1)S(1)}, bf16[16,104,128]{2,1,0:T(8,128)(2,1)S(1)}, u32[]{:S(2)}, u32[]{:S(2)}) collective-permute-start(bf16[16,104,128]{2,1,0:T(8,128)(2,1)S(1)} %get-tuple-element.58), channel_id=1, source_target_pairs={{0,3},{1,2},{2,1},{3,0},{4,7},{5,6},{6,5},{7,4},{8,11},{9,10},{10,... | collective-permute-start | bytes 1277960 | tf_op jit(solution)/shard_map/ppermute | solution.py:47
  95.7 11.6 %collective-permute-start.19 = (bf16[16,104,128]{2,1,0:T(8,128)(2,1)S(1)}, bf16[16,104,128]{2,1,0:T(8,128)(2,1)S(1)}, u32[]{:S(2)}, u32[]{:S(2)}) collective-permute-start(bf16[16,104,128]{2,1,0:T(8,128)(2,1)S(1)} %get-tuple-element.60), channel_id=1, source_target_pairs={{0,4},{1,5},{2,6},{3,7},{4,0},{5,1},{6,2},{7,3},{8,12},{9,13},{10,... | collective-permute-start | bytes 1277960 | tf_op jit(solution)/shard_map/ppermute | solution.py:47
  97.8 12.5 %collective-permute-start.3 = (bf16[16,104,128]{2,1,0:T(8,128)(2,1)S(1)}, bf16[16,104,128]{2,1,0:T(8,128)(2,1)S(1)}, u32[]{:S(2)}, u32[]{:S(2)}) collective-permute-start(bf16[16,104,128]{2,1,0:T(8,128)(2,1)S(1)} %get-tuple-element.56), channel_id=1, source_target_pairs={{0,12},{1,13},{2,14},{3,15},{4,8},{5,9},{6,10},{7,11},{8,4},{9,5},... | collective-permute-start | bytes 1277960 | tf_op jit(solution)/shard_map/ppermute | solution.py:47
  100.2 12.4 %collective-permute-start.28 = (bf16[8,104,128]{2,1,0:T(8,128)(2,1)S(1)}, bf16[8,104,128]{2,1,0:T(8,128)(2,1)S(1)}, u32[]{:S(2)}, u32[]{:S(2)}) collective-permute-start(bf16[8,104,128]{2,1,0:T(8,128)(2,1)S(1)} %get-tuple-element.112), channel_id=1, source_target_pairs={{0,12},{1,13},{2,14},{3,15},{4,8},{5,9},{6,10},{7,11},{8,4},{9,5},... | collective-permute-start | bytes 638984 | tf_op jit(solution)/shard_map/ppermute | solution.py:47
  105.1 9.4 %collective-permute-start.12 = (bf16[8,104,128]{2,1,0:T(8,128)(2,1)S(1)}, bf16[8,104,128]{2,1,0:T(8,128)(2,1)S(1)}, u32[]{:S(2)}, u32[]{:S(2)}) collective-permute-start(bf16[8,104,128]{2,1,0:T(8,128)(2,1)S(1)} %get-tuple-element.116), channel_id=1, source_target_pairs={{0,4},{1,5},{2,6},{3,7},{4,0},{5,1},{6,2},{7,3},{8,12},{9,13},{10,... | collective-permute-start | bytes 638984 | tf_op jit(solution)/shard_map/ppermute | solution.py:47
  114.7 8.2 %collective-permute-start.21 = (bf16[4,104,128]{2,1,0:T(8,128)(2,1)S(1)}, bf16[4,104,128]{2,1,0:T(8,128)(2,1)S(1)}, u32[]{:S(2)}, u32[]{:S(2)}) collective-permute-start(bf16[4,104,128]{2,1,0:T(8,128)(2,1)S(1)} %get-tuple-element.130), channel_id=1, source_target_pairs={{0,12},{1,13},{2,14},{3,15},{4,8},{5,9},{6,10},{7,11},{8,4},{9,5},... | collective-permute-start | bytes 319496 | tf_op jit(solution)/shard_map/ppermute | solution.py:47
  141.7 11.7 %collective-permute-start.17 = (bf16[8,104,128]{2,1,0:T(8,128)(2,1)S(1)}, bf16[8,104,128]{2,1,0:T(8,128)(2,1)S(1)}, u32[]{:S(2)}, u32[]{:S(2)}) collective-permute-start(bf16[8,104,128]{2,1,0:T(8,128)(2,1)S(1)} %pad_maximum_fusion.17), channel_id=1, source_target_pairs={{0,4},{1,5},{2,6},{3,7},{4,0},{5,1},{6,2},{7,3},{8,12},{9,13},{10,... | collective-permute-start | bytes 638984 | tf_op jit(solution)/shard_map/ppermute | solution.py:47
  147.7 18.5 %collective-permute-start.10 = (bf16[16,104,128]{2,1,0:T(8,128)(2,1)S(1)}, bf16[16,104,128]{2,1,0:T(8,128)(2,1)S(1)}, u32[]{:S(2)}, u32[]{:S(2)}) collective-permute-start(bf16[16,104,128]{2,1,0:T(8,128)(2,1)S(1)} %pad_maximum_fusion.4.rest_0_), channel_id=1, source_target_pairs={{0,12},{1,13},{2,14},{3,15},{4,8},{5,9},{6,10},{7,11},{8,4},{9,5},... | collective-permute-start | bytes 1277960 | tf_op jit(solution)/shard_map/ppermute | solution.py:47
  151.4 8.2 %collective-permute-start.26 = (bf16[16,104,128]{2,1,0:T(8,128)(2,1)S(1)}, bf16[16,104,128]{2,1,0:T(8,128)(2,1)S(1)}, u32[]{:S(2)}, u32[]{:S(2)}) collective-permute-start(bf16[16,104,128]{2,1,0:T(8,128)(2,1)S(1)} %pad_maximum_fusion.6.rest_0_), channel_id=1, source_target_pairs={{0,4},{1,5},{2,6},{3,7},{4,0},{5,1},{6,2},{7,3},{8,12},{9,13},{10,... | collective-permute-start | bytes 1277960 | tf_op jit(solution)/shard_map/ppermute | solution.py:47
  152.2 8.2 %collective-permute-start.34 = (bf16[16,104,128]{2,1,0:T(8,128)(2,1)S(1)}, bf16[16,104,128]{2,1,0:T(8,128)(2,1)S(1)}, u32[]{:S(2)}, u32[]{:S(2)}) collective-permute-start(bf16[16,104,128]{2,1,0:T(8,128)(2,1)S(1)} %pad_maximum_fusion.7.rest_2_), channel_id=1, source_target_pairs={{0,1},{1,0},{2,3},{3,2},{4,5},{5,4},{6,7},{7,6},{8,9},{9,8},{10,11... | collective-permute-start | bytes 1277960 | tf_op jit(solution)/shard_map/ppermute | solution.py:47
  153.4 12.8 %collective-permute-start.18 = (bf16[16,104,128]{2,1,0:T(8,128)(2,1)S(1)}, bf16[16,104,128]{2,1,0:T(8,128)(2,1)S(1)}, u32[]{:S(2)}, u32[]{:S(2)}) collective-permute-start(bf16[16,104,128]{2,1,0:T(8,128)(2,1)S(1)} %pad_maximum_fusion.5.rest_2_), channel_id=1, source_target_pairs={{0,3},{1,2},{2,1},{3,0},{4,7},{5,6},{6,5},{7,4},{8,11},{9,10},{10,... | collective-permute-start | bytes 1277960 | tf_op jit(solution)/shard_map/ppermute | solution.py:47
  173.6 9.4 %collective-permute-start.36 = (bf16[16,104,128]{2,1,0:T(8,128)(2,1)S(1)}, bf16[16,104,128]{2,1,0:T(8,128)(2,1)S(1)}, u32[]{:S(2)}, u32[]{:S(2)}) collective-permute-start(bf16[16,104,128]{2,1,0:T(8,128)(2,1)S(1)} %slice.845), channel_id=1, source_target_pairs={{0,96},{1,97},{2,98},{3,99},{4,100},{5,101},{6,102},{7,103},{8,104... | collective-permute-start | bytes 1277960 | tf_op jit(solution)/shard_map/ppermute | solution.py:47
  195.2 9.4 %collective-permute-start.39 = (bf16[16,104,128]{2,1,0:T(8,128)(2,1)S(1)}, bf16[16,104,128]{2,1,0:T(8,128)(2,1)S(1)}, u32[]{:S(2)}, u32[]{:S(2)}) collective-permute-start(bf16[16,104,128]{2,1,0:T(8,128)(2,1)S(1)} %pad_maximum_fusion.8), channel_id=1, source_target_pairs={{0,96},{1,97},{2,98},{3,99},{4,100},{5,101},{6,102},{7,103},{8,104... | collective-permute-start | bytes 1277960 | tf_op jit(solution)/shard_map/ppermute | solution.py:47
  213.2 11.4 %collective-permute-start.65 = (bf16[16,104,128]{2,1,0:T(8,128)(2,1)S(1)}, bf16[16,104,128]{2,1,0:T(8,128)(2,1)S(1)}, u32[]{:S(2)}, u32[]{:S(2)}) collective-permute-start(bf16[16,104,128]{2,1,0:T(8,128)(2,1)S(1)} %get-tuple-element.72), channel_id=1, source_target_pairs={{0,1},{1,0},{2,3},{3,2},{4,5},{5,4},{6,7},{7,6},{8,9},{9,8},{10,11... | collective-permute-start | bytes 1277960 | tf_op jit(solution)/shard_map/ppermute | solution.py:47
  214.0 12.2 %collective-permute-start.57 = (bf16[16,104,128]{2,1,0:T(8,128)(2,1)S(1)}, bf16[16,104,128]{2,1,0:T(8,128)(2,1)S(1)}, u32[]{:S(2)}, u32[]{:S(2)}) collective-permute-start(bf16[16,104,128]{2,1,0:T(8,128)(2,1)S(1)} %get-tuple-element.70), channel_id=1, source_target_pairs={{0,4},{1,5},{2,6},{3,7},{4,0},{5,1},{6,2},{7,3},{8,12},{9,13},{10,... | collective-permute-start | bytes 1277960 | tf_op jit(solution)/shard_map/ppermute | solution.py:47
  219.5 13.0 %collective-permute-start.49 = (bf16[16,104,128]{2,1,0:T(8,128)(2,1)S(1)}, bf16[16,104,128]{2,1,0:T(8,128)(2,1)S(1)}, u32[]{:S(2)}, u32[]{:S(2)}) collective-permute-start(bf16[16,104,128]{2,1,0:T(8,128)(2,1)S(1)} %get-tuple-element.68), channel_id=1, source_target_pairs={{0,3},{1,2},{2,1},{3,0},{4,7},{5,6},{6,5},{7,4},{8,11},{9,10},{10,... | collective-permute-start | bytes 1277960 | tf_op jit(solution)/shard_map/ppermute | solution.py:47
  222.3 13.6 %collective-permute-start.41 = (bf16[16,104,128]{2,1,0:T(8,128)(2,1)S(1)}, bf16[16,104,128]{2,1,0:T(8,128)(2,1)S(1)}, u32[]{:S(2)}, u32[]{:S(2)}) collective-permute-start(bf16[16,104,128]{2,1,0:T(8,128)(2,1)S(1)} %get-tuple-element.66), channel_id=1, source_target_pairs={{0,12},{1,13},{2,14},{3,15},{4,8},{5,9},{6,10},{7,11},{8,4},{9,5},... | collective-permute-start | bytes 1277960 | tf_op jit(solution)/shard_map/ppermute | solution.py:47
  224.6 13.5 %collective-permute-start.66 = (bf16[8,104,128]{2,1,0:T(8,128)(2,1)S(1)}, bf16[8,104,128]{2,1,0:T(8,128)(2,1)S(1)}, u32[]{:S(2)}, u32[]{:S(2)}) collective-permute-start(bf16[8,104,128]{2,1,0:T(8,128)(2,1)S(1)} %get-tuple-element.104), channel_id=1, source_target_pairs={{0,12},{1,13},{2,14},{3,15},{4,8},{5,9},{6,10},{7,11},{8,4},{9,5},... | collective-permute-start | bytes 638984 | tf_op jit(solution)/shard_map/ppermute | solution.py:47
  226.2 14.0 %collective-permute-start.58 = (bf16[8,104,128]{2,1,0:T(8,128)(2,1)S(1)}, bf16[8,104,128]{2,1,0:T(8,128)(2,1)S(1)}, u32[]{:S(2)}, u32[]{:S(2)}) collective-permute-start(bf16[8,104,128]{2,1,0:T(8,128)(2,1)S(1)} %get-tuple-element.106), channel_id=1, source_target_pairs={{0,1},{1,0},{2,3},{3,2},{4,5},{5,4},{6,7},{7,6},{8,9},{9,8},{10,11... | collective-permute-start | bytes 638984 | tf_op jit(solution)/shard_map/ppermute | solution.py:47
  232.6 9.7 %collective-permute-start.50 = (bf16[8,104,128]{2,1,0:T(8,128)(2,1)S(1)}, bf16[8,104,128]{2,1,0:T(8,128)(2,1)S(1)}, u32[]{:S(2)}, u32[]{:S(2)}) collective-permute-start(bf16[8,104,128]{2,1,0:T(8,128)(2,1)S(1)} %get-tuple-element.108), channel_id=1, source_target_pairs={{0,4},{1,5},{2,6},{3,7},{4,0},{5,1},{6,2},{7,3},{8,12},{9,13},{10,... | collective-permute-start | bytes 638984 | tf_op jit(solution)/shard_map/ppermute | solution.py:47
  267.4 11.5 %collective-permute-start.55 = (bf16[8,104,128]{2,1,0:T(8,128)(2,1)S(1)}, bf16[8,104,128]{2,1,0:T(8,128)(2,1)S(1)}, u32[]{:S(2)}, u32[]{:S(2)}) collective-permute-start(bf16[8,104,128]{2,1,0:T(8,128)(2,1)S(1)} %pad_maximum_fusion.21), channel_id=1, source_target_pairs={{0,4},{1,5},{2,6},{3,7},{4,0},{5,1},{6,2},{7,3},{8,12},{9,13},{10,... | collective-permute-start | bytes 638984 | tf_op jit(solution)/shard_map/ppermute | solution.py:47
  269.4 8.2 %collective-permute-start.63 = (bf16[8,104,128]{2,1,0:T(8,128)(2,1)S(1)}, bf16[8,104,128]{2,1,0:T(8,128)(2,1)S(1)}, u32[]{:S(2)}, u32[]{:S(2)}) collective-permute-start(bf16[8,104,128]{2,1,0:T(8,128)(2,1)S(1)} %pad_maximum_fusion.22), channel_id=1, source_target_pairs={{0,1},{1,0},{2,3},{3,2},{4,5},{5,4},{6,7},{7,6},{8,9},{9,8},{10,11... | collective-permute-start | bytes 638984 | tf_op jit(solution)/shard_map/ppermute | solution.py:47
  270.0 7.9 %collective-permute-start.71 = (bf16[8,104,128]{2,1,0:T(8,128)(2,1)S(1)}, bf16[8,104,128]{2,1,0:T(8,128)(2,1)S(1)}, u32[]{:S(2)}, u32[]{:S(2)}) collective-permute-start(bf16[8,104,128]{2,1,0:T(8,128)(2,1)S(1)} %pad_maximum_fusion.23), channel_id=1, source_target_pairs={{0,12},{1,13},{2,14},{3,15},{4,8},{5,9},{6,10},{7,11},{8,4},{9,5},... | collective-permute-start | bytes 638984 | tf_op jit(solution)/shard_map/ppermute | solution.py:47
  272.8 19.1 %collective-permute-start.48 = (bf16[16,104,128]{2,1,0:T(8,128)(2,1)S(1)}, bf16[16,104,128]{2,1,0:T(8,128)(2,1)S(1)}, u32[]{:S(2)}, u32[]{:S(2)}) collective-permute-start(bf16[16,104,128]{2,1,0:T(8,128)(2,1)S(1)} %pad_maximum_fusion.9.rest_0_), channel_id=1, source_target_pairs={{0,12},{1,13},{2,14},{3,15},{4,8},{5,9},{6,10},{7,11},{8,4},{9,5},... | collective-permute-start | bytes 1277960 | tf_op jit(solution)/shard_map/ppermute | solution.py:47
  277.7 8.2 %collective-permute-start.64 = (bf16[16,104,128]{2,1,0:T(8,128)(2,1)S(1)}, bf16[16,104,128]{2,1,0:T(8,128)(2,1)S(1)}, u32[]{:S(2)}, u32[]{:S(2)}) collective-permute-start(bf16[16,104,128]{2,1,0:T(8,128)(2,1)S(1)} %pad_maximum_fusion.11.rest_0_), channel_id=1, source_target_pairs={{0,4},{1,5},{2,6},{3,7},{4,0},{5,1},{6,2},{7,3},{8,12},{9,13},{10,... | collective-permute-start | bytes 1277960 | tf_op jit(solution)/shard_map/ppermute | solution.py:47
  277.9 8.2 %collective-permute-start.72 = (bf16[16,104,128]{2,1,0:T(8,128)(2,1)S(1)}, bf16[16,104,128]{2,1,0:T(8,128)(2,1)S(1)}, u32[]{:S(2)}, u32[]{:S(2)}) collective-permute-start(bf16[16,104,128]{2,1,0:T(8,128)(2,1)S(1)} %pad_maximum_fusion.12.rest_2_), channel_id=1, source_target_pairs={{0,1},{1,0},{2,3},{3,2},{4,5},{5,4},{6,7},{7,6},{8,9},{9,8},{10,11... | collective-permute-start | bytes 1277960 | tf_op jit(solution)/shard_map/ppermute | solution.py:47
  278.9 13.0 %collective-permute-start.56 = (bf16[16,104,128]{2,1,0:T(8,128)(2,1)S(1)}, bf16[16,104,128]{2,1,0:T(8,128)(2,1)S(1)}, u32[]{:S(2)}, u32[]{:S(2)}) collective-permute-start(bf16[16,104,128]{2,1,0:T(8,128)(2,1)S(1)} %pad_maximum_fusion.10.rest_2_), channel_id=1, source_target_pairs={{0,3},{1,2},{2,1},{3,0},{4,7},{5,6},{6,5},{7,4},{8,11},{9,10},{10,... | collective-permute-start | bytes 1277960 | tf_op jit(solution)/shard_map/ppermute | solution.py:47
  299.3 9.4 %collective-permute-start.74 = (bf16[16,104,128]{2,1,0:T(8,128)(2,1)S(1)}, bf16[16,104,128]{2,1,0:T(8,128)(2,1)S(1)}, u32[]{:S(2)}, u32[]{:S(2)}) collective-permute-start(bf16[16,104,128]{2,1,0:T(8,128)(2,1)S(1)} %slice.844), channel_id=1, source_target_pairs={{0,96},{1,97},{2,98},{3,99},{4,100},{5,101},{6,102},{7,103},{8,104... | collective-permute-start | bytes 1277960 | tf_op jit(solution)/shard_map/ppermute | solution.py:47
  (48 other events, 331.9 us)
where the time goes:
time: 316 us
  waiting for transfers between devices  146 us (46%)
  starting transfers between devices  94.8 us (30%)
  Pallas kernels  48.2 us (15%)
  other arithmetic  11.8 us (4%)
  local copies, waits for them, and re-layouts  10.1 us (3%)
  between operations  5.39 us (2%)
    ppermute x76, waiting for transfers between devices, swap(): return lax.ppermute(value, AXES, pairs)  108 us
    ppermute x76, starting transfers between devices, swap(): return lax.ppermute(value, AXES, pairs)  90.2 us
    all_to_all x1, waiting for transfers between devices, move(): lax.all_to_all(packed, 'ice', split_axis=0, concat_axis=0, tiled=True)  37.5 us
    pallas_call x4, Pallas kernels, forward(): pl.pallas_call(forward_kernel, in_specs=[SMEM_SPEC] * TABLES + [VMEM_SPEC...  21 us
    pallas_call x2, Pallas kernels, first_backward(): pl.pallas_call(first_backward_kernel, in_specs=[SMEM_SPEC] * TABLES + [VM...  11.5 us
    pallas_call x2, Pallas kernels, last_backward(): pl.pallas_call(last_backward_kernel, in_specs=[SMEM_SPEC] * TABLES + [VME...  9.35 us
    pallas_call x1, Pallas kernels, pack(): pl.pallas_call(pack_kernel, grid_spec=pltpu.PrefetchScalarGridSpec(num_sc...  6.37 us
  transfers between devices with their start and end apart: 77, of which 43 were waited for; matrix products, arithmetic and copies ran while one was open for 4% of the time, Pallas kernels for 9%

commit v1 on v0

--- a/solution.py
+++ b/solution.py
@@ -18,6 +18,7 @@
 HALVES = 2
 DIMS = {"x1": (0, 1), "x3": (0, 3), "c": (1, 1), "z1": (2, 1), "z3": (2, 3), "y1": (3, 1), "y3": (3, 3)}
 OCN_DIMS = ("z1", "y1", "z3", "y3")
+ORDERS = (("z1", "z3", "y1", "y3"), ("z3", "z1", "y1", "y3"), ("y1", "y3", "z1", "z3"), ("y3", "y1", "z1", "z3"))
 ICE_DIMS = ("x1", "x3")
 COLOURS = 4
 PER = 8 // COLOURS
@@ -26,7 +27,7 @@
 
 
 def ocn_dim(colour, step):
-    return OCN_DIMS[(colour + step) % 4]
+    return ORDERS[colour][step]
 
 
 def ice_dim(core, step):
@@ -292,20 +293,34 @@
     return part
 
 
-def scatter_ocn(send, keep, colour):
-    got = swap_ocn(send, colour, 0)
-    for step in range(1, 4):
-        n = keep.shape[0] // 2
-        send = (keep[n:] + got[n:].astype(F32)).astype(BF)
-        keep = keep[:n] + got[:n].astype(F32)
-        got = swap_ocn(send, colour, step)
+def halve(keep, got, axis):
+    n = keep.shape[axis] // 2
+    low, high = (lambda v: lax.slice_in_dim(v, 0, n, axis=axis)), (lambda v: lax.slice_in_dim(v, n, 2 * n, axis=axis))
+    return low(keep) + low(got).astype(F32), (high(keep) + high(got).astype(F32)).astype(BF)
+
+
+def scatter_ocn(sends, keeps, half):
+    parts = []
+    for i in range(2):
+        k = 2 * half + i
+        keep, send = halve(keeps[i], swap_ocn(sends[i], k, 0), 0)
+        parts.append((keep, swap_ocn(send, k, 1)))
+    keep, got = (jnp.stack([part[j] for part in parts]) for j in range(2))
+    for step in (2, 3):
+        keep, send = halve(keep, got, 1)
+        got = swap_ocn(send, 2 * half, step)
     return keep + got.astype(F32)
 
 
-def gather_ocn(own, colour):
-    for step in (3, 2, 1):
-        own = jnp.concatenate([own, swap_ocn(own, colour, step)], 0)
-    return [own, swap_ocn(own, colour, 0)]
+def gather_ocn(own, half):
+    for step in (3, 2):
+        own = jnp.concatenate([own, swap_ocn(own, 2 * half, step)], 1)
+    pieces = []
+    for i in range(2):
+        k = 2 * half + i
+        line = jnp.concatenate([own[i], swap_ocn(own[i], k, 1)], 0)
+        pieces += [line, swap_ocn(line, k, 0)]
+    return pieces
 
 
 def bit_of(displacement, name):
@@ -434,16 +449,15 @@
         flux = []
         for h in range(HALVES):
             sends, keeps = forward(tables[h], ice_all, moved, late)
-            for i in range(2):
-                k = 2 * h + i
-                total = scatter_ocn(sends[i], keeps[i], k)
-                flux.append(jnp.tanh(total + ocean[PER * k : PER * (k + 1)].astype(F32)).astype(BF))
-        pieces = [gather_ocn(flux[k], k) for k in range(COLOURS)]
-        so_far = first_backward(tables[0], pieces[0] + pieces[1], moved, late)
-        send, keep = last_backward(tables[1], pieces[2] + pieces[3], so_far, moved, late)
+            total = scatter_ocn(sends, keeps, h)
+            state = ocean[4 * h : 4 * h + 4].reshape(total.shape)
+            flux.append(jnp.tanh(total + state.astype(F32)).astype(BF))
+        pieces = [gather_ocn(flux[h], h) for h in range(HALVES)]
+        so_far = first_backward(tables[0], pieces[0], moved, late)
+        send, keep = last_backward(tables[1], pieces[1], so_far, moved, late)
         forcing = scatter_ice(send, keep)
         ice = (land * (ice.astype(F32) + rates * jnp.tanh(forcing))).astype(BF)
-    return untiled(ice), untiled(jnp.concatenate(flux, 0))
+    return untiled(ice), untiled(jnp.concatenate(flux, 0).reshape(8, ROWS, 128))
 
 
 def solution(mesh):

time: 316 us -> 314 us (level)
  starting transfers between devices: 94.8 us -> 69 us
  waiting for transfers between devices: 146 us -> 167 us
    ppermute x76 -> x60, starting transfers between devices: 90.2 us -> 64.4 us  [swap(): return lax.ppermute(value, AXES, pairs)]
    ppermute x76 -> x60, waiting for transfers between devices: 108 us -> 125 us  [swap(): return lax.ppermute(value, AXES, pairs)]
    all_to_all x1, waiting for transfers between devices: 37.5 us -> 41.5 us  [move(): lax.all_to_all(packed, 'ice', split_axis=0, concat_axis=0, tiled=True)]
  transfers between devices with their start and end apart: 77 -> 61, of which waited for: 43 -> 41; matrix products, arithmetic and copies ran while one was open for 4% -> 4% of each run, Pallas kernels for 9% -> 9%
where the time goes in v1:
time: 314 us; the launch traced here: 313 us
  waiting for transfers between devices  167 us (53%)
  starting transfers between devices  69 us (22%)
  Pallas kernels  49.2 us (16%)
  other arithmetic  13.8 us (4%)
  local copies, waits for them, and re-layouts  8.96 us (3%)
  between operations  5.21 us (2%)
    ppermute x60, waiting for transfers between devices, swap(): return lax.ppermute(value, AXES, pairs)  125 us
    ppermute x60, starting transfers between devices, swap(): return lax.ppermute(value, AXES, pairs)  64.4 us
    all_to_all x1, waiting for transfers between devices, move(): lax.all_to_all(packed, 'ice', split_axis=0, concat_axis=0, tiled=True)  41.5 us
    pallas_call x4, Pallas kernels, forward(): pl.pallas_call(forward_kernel, in_specs=[SMEM_SPEC] * TABLES + [VMEM_SPEC...  21.9 us
    pallas_call x2, Pallas kernels, first_backward(): pl.pallas_call(first_backward_kernel, in_specs=[SMEM_SPEC] * TABLES + [VM...  11.5 us
    pallas_call x2, Pallas kernels, last_backward(): pl.pallas_call(last_backward_kernel, in_specs=[SMEM_SPEC] * TABLES + [VME...  9.36 us
    pallas_call x1, Pallas kernels, pack(): pl.pallas_call(pack_kernel, grid_spec=pltpu.PrefetchScalarGridSpec(num_sc...  6.37 us
  transfers between devices with their start and end apart: 61, of which 41 were waited for; matrix products, arithmetic and copies ran while one was open for 4% of the time, Pallas kernels for 9%

profile of v1, /device:TPU:0, one launch (start us, length us, event | category | flops | bytes accessed | tf_op | source)
XLA Modules:
  0.0 313.0 jit_solution(17728572160086803266)
XLA Ops:
  8.7 6.4 %pack_rows.3 = bf16[1056,16,128]{2,1,0:T(8,128)(2,1)S(1)} custom-call(s32[128]{0:T(128)S(1)} %get-tuple-element.151.base_ref, s32[128]{0:T(128)} %valid_ref.1, bf16[128,128,128]{2,1,0:T(8,128)(2,1)} %w_ref.1), custom_call_target="tpu_custom_call" | custom-call | tf_op jit(solution)/shard_map/pack_rows/pallas_call | solution.py:89
  19.9 7.2 %collective-permute-done.1 = bf16[16,104,128]{2,1,0:T(8,128)(2,1)S(1)} collective-permute-done((bf16[16,104,128]{2,1,0:T(8,128)(2,1)S(1)}, bf16[16,104,128]{2,1,0:T(8,128)(2,1)S(1)}, u32[]{:S(2)}, u32[]{:S(2)}) %collective-permute-start.1) | collective-permute-done | bytes 426016 | tf_op jit(solution)/shard_map/ppermute | solution.py:48
  28.1 4.5 %all-to-all-start.1 = ((bf16[8,1984,128]{2,1,0:T(8,128)(2,1)}), bf16[8,1984,128]{2,1,0:T(8,128)(2,1)}, u32[]{:S(2)}, u32[]{:S(2)}) async-start(bf16[8,1984,128]{2,1,0:T(8,128)(2,1)} %bitcast.276), calls=%async_computation.1 | async-start | bytes 8126464 | tf_op jit(solution)/shard_map/all_to_all | solution.py:338
  39.5 41.5 %all-to-all-done.1 = bf16[8,1984,128]{2,1,0:T(8,128)(2,1)} async-done(((bf16[8,1984,128]{2,1,0:T(8,128)(2,1)}), bf16[8,1984,128]{2,1,0:T(8,128)(2,1)}, u32[]{:S(2)}, u32[]{:S(2)}) %all-to-all-start.1) | async-done | bytes 4063264 | tf_op jit(solution)/shard_map/all_to_all | solution.py:338
  81.0 6.8 %products.5 = (bf16[16,104,128]{2,1,0:T(8,128)(2,1)}, bf16[16,104,128]{2,1,0:T(8,128)(2,1)}, f32[16,104,128]{2,1,0:T(8,128)S(1)}, f32[16,104,128]{2,1,0:T(8,128)S(1)}) custom-call(s32[272]{0:T(512)S(1)} %get-tuple-element.79.list_ref, s32[11]{0:T(128)S(1)} %get-tuple-element.153.counts_ref, ...), custom_call_target="tpu_custom_call" | custom-call | tf_op jit(solution)/shard_map/products/pallas_call | solution.py:215
  94.4 4.6 %products.4 = (bf16[16,104,128]{2,1,0:T(8,128)(2,1)S(1)}, bf16[16,104,128]{2,1,0:T(8,128)(2,1)S(1)}, f32[16,104,128]{2,1,0:T(8,128)S(1)}, f32[16,104,128]{2,1,0:T(8,128)S(1)}) custom-call(s32[272]{0:T(512)S(1)} %get-tuple-element.80.list_ref, s32[11]{0:T(128)S(1)} %get-tuple-element.154.counts_ref, ...), custom_call_target="tpu_custom_call" | custom-call | tf_op jit(solution)/shard_map/products/pallas_call | solution.py:215
  107.1 3.2 %collective-permute-done.3 = bf16[16,104,128]{2,1,0:T(8,128)(2,1)S(1)} collective-permute-done((bf16[16,104,128]{2,1,0:T(8,128)(2,1)S(1)}, bf16[16,104,128]{2,1,0:T(8,128)(2,1)S(1)}, u32[]{:S(2)}, u32[]{:S(2)}) %collective-permute-start.3) | collective-permute-done | bytes 426016 | tf_op jit(solution)/shard_map/ppermute | solution.py:48
  110.3 2.9 collective-permute-start.5
  117.5 2.9 collective-permute-done.6
  135.3 5.0 %collective-permute-done.9 = bf16[2,2,104,128]{3,2,1,0:T(8,128)(2,1)S(1)} collective-permute-done((bf16[2,2,104,128]{3,2,1,0:T(8,128)(2,1)S(1)}, bf16[2,2,104,128]{3,2,1,0:T(8,128)(2,1)S(1)}, u32[]{:S(2)}, u32[]{:S(2)}) %collective-permute-start.9) | collective-permute-done | bytes 106528 | tf_op jit(solution)/shard_map/ppermute | solution.py:48
  145.3 2.9 collective-permute-done.10
  149.0 3.7 %collective-permute-done.25 = bf16[8,104,128]{2,1,0:T(8,128)(2,1)S(1)} collective-permute-done((bf16[8,104,128]{2,1,0:T(8,128)(2,1)S(1)}, bf16[8,104,128]{2,1,0:T(8,128)(2,1)S(1)}, u32[]{:S(2)}, u32[]{:S(2)}) %collective-permute-start.25) | collective-permute-done | bytes 213024 | tf_op jit(solution)/shard_map/ppermute | solution.py:48
  156.3 5.9 %collective-permute-done.26.rest_3_ = bf16[16,104,128]{2,1,0:T(8,128)(2,1)S(1)} collective-permute-done((bf16[16,104,128]{2,1,0:T(8,128)(2,1)S(1)}, bf16[16,104,128]{2,1,0:T(8,128)(2,1)S(1)}, u32[]{:S(2)}, u32[]{:S(2)}) %collective-permute-start.26) | collective-permute-done | bytes 426016 | tf_op jit(solution)/shard_map/ppermute | solution.py:48
  162.2 5.8 %returns.4.rest_4_ = f32[64,104,128]{2,1,0:T(8,128)S(1)} custom-call(s32[272]{0:T(512)S(1)} %get-tuple-element.79.list_ref, s32[11]{0:T(128)S(1)} %get-tuple-element.153.counts_ref, bf16[16,104,128]{2,1,0:T(8,128)(2,1)S(1)} %pad_maximum_fusion.12.rest_0_, bf16[16,104,128]{2,1,0:T(8,128)(2,1)S(1)} %collective-permute-done.24.rest_1_, ...), custom_call_target="tpu_custom_call" | custom-call | tf_op jit(solution)/shard_map/returns/pallas_call | solution.py:237
  168.0 4.7 %returns.5 = (bf16[32,104,128]{2,1,0:T(8,128)(2,1)S(1)}, f32[32,104,128]{2,1,0:T(8,128)S(1)}) custom-call(s32[272]{0:T(512)S(1)} %get-tuple-element.80.list_ref, s32[11]{0:T(128)S(1)} %get-tuple-element.154.counts_ref, bf16[16,104,128]{2,1,0:T(8,128)(2,1)S(1)} %pad_maximum_fusion.9.rest_0_, bf16[16,104,128]{2,1,0:T(8,128)(2,1)S(1)} %collective-permute-done.12.rest_1_, ...), custom_call_target="tpu_custom_call" | custom-call | tf_op jit(solution)/shard_map/returns/pallas_call | solution.py:260
  175.5 9.3 %collective-permute-done.28 = bf16[16,104,128]{2,1,0:T(8,128)(2,1)S(1)} collective-permute-done((bf16[16,104,128]{2,1,0:T(8,128)(2,1)S(1)}, bf16[16,104,128]{2,1,0:T(8,128)(2,1)S(1)}, u32[]{:S(2)}, u32[]{:S(2)}) %collective-permute-start.28) | collective-permute-done | bytes 426016 | tf_op jit(solution)/shard_map/ppermute | solution.py:48
  185.1 5.7 %collective-permute-done.29 = bf16[8,104,128]{2,1,0:T(8,128)(2,1)S(1)} collective-permute-done((bf16[8,104,128]{2,1,0:T(8,128)(2,1)S(1)}, bf16[8,104,128]{2,1,0:T(8,128)(2,1)S(1)}, u32[]{:S(2)}, u32[]{:S(2)}) %collective-permute-start.29) | collective-permute-done | bytes 213024 | tf_op jit(solution)/shard_map/ppermute | solution.py:48
  191.1 5.8 %collective-permute-done.30 = bf16[8,104,128]{2,1,0:T(8,128)(2,1)S(1)} collective-permute-done((bf16[8,104,128]{2,1,0:T(8,128)(2,1)S(1)}, bf16[8,104,128]{2,1,0:T(8,128)(2,1)S(1)}, u32[]{:S(2)}, u32[]{:S(2)}) %collective-permute-start.30) | collective-permute-done | bytes 213024 | tf_op jit(solution)/shard_map/ppermute | solution.py:48
  197.1 9.3 %collective-permute-done.31 = bf16[16,104,128]{2,1,0:T(8,128)(2,1)S(1)} collective-permute-done((bf16[16,104,128]{2,1,0:T(8,128)(2,1)S(1)}, bf16[16,104,128]{2,1,0:T(8,128)(2,1)S(1)}, u32[]{:S(2)}, u32[]{:S(2)}) %collective-permute-start.31) | collective-permute-done | bytes 426016 | tf_op jit(solution)/shard_map/ppermute | solution.py:48
  209.1 5.9 %products.7 = (bf16[16,104,128]{2,1,0:T(8,128)(2,1)S(1)}, bf16[16,104,128]{2,1,0:T(8,128)(2,1)S(1)}, f32[16,104,128]{2,1,0:T(8,128)S(1)}, f32[16,104,128]{2,1,0:T(8,128)S(1)}) custom-call(s32[272]{0:T(512)S(1)} %get-tuple-element.79.list_ref, s32[11]{0:T(128)S(1)} %get-tuple-element.153.counts_ref, bf16[64,104,128]{2,1,0:T(8,128)(2,1)S(1)} %pad_maximum_fusion.rest_0_, ...), custom_call_target="tpu_custom_call" | custom-call | tf_op jit(solution)/shard_map/products/pallas_call | solution.py:215
  216.7 4.6 %products.6 = (bf16[16,104,128]{2,1,0:T(8,128)(2,1)S(1)}, bf16[16,104,128]{2,1,0:T(8,128)(2,1)S(1)}, f32[16,104,128]{2,1,0:T(8,128)S(1)}, f32[16,104,128]{2,1,0:T(8,128)S(1)}) custom-call(s32[272]{0:T(512)S(1)} %get-tuple-element.80.list_ref, s32[11]{0:T(128)S(1)} %get-tuple-element.154.counts_ref, bf16[64,104,128]{2,1,0:T(8,128)(2,1)S(1)} %pad_maximum_fusion.rest_0_, ...), custom_call_target="tpu_custom_call" | custom-call | tf_op jit(solution)/shard_map/products/pallas_call | solution.py:215
  228.7 4.4 %collective-permute-done.33 = bf16[16,104,128]{2,1,0:T(8,128)(2,1)S(1)} collective-permute-done((bf16[16,104,128]{2,1,0:T(8,128)(2,1)S(1)}, bf16[16,104,128]{2,1,0:T(8,128)(2,1)S(1)}, u32[]{:S(2)}, u32[]{:S(2)}) %collective-permute-start.33) | collective-permute-done | bytes 426016 | tf_op jit(solution)/shard_map/ppermute | solution.py:48
  237.1 3.7 %collective-permute-done.35 = bf16[8,104,128]{2,1,0:T(8,128)(2,1)S(1)} collective-permute-done((bf16[8,104,128]{2,1,0:T(8,128)(2,1)S(1)}, bf16[8,104,128]{2,1,0:T(8,128)(2,1)S(1)}, u32[]{:S(2)}, u32[]{:S(2)}) %collective-permute-start.35) | collective-permute-done | bytes 213024 | tf_op jit(solution)/shard_map/ppermute | solution.py:48
  254.6 2.8 collective-permute-start.39
  257.5 3.3 %collective-permute-done.39 = bf16[2,2,104,128]{3,2,1,0:T(8,128)(2,1)S(1)} collective-permute-done((bf16[2,2,104,128]{3,2,1,0:T(8,128)(2,1)S(1)}, bf16[2,2,104,128]{3,2,1,0:T(8,128)(2,1)S(1)}, u32[]{:S(2)}, u32[]{:S(2)}) %collective-permute-start.39) | collective-permute-done | bytes 106528 | tf_op jit(solution)/shard_map/ppermute | solution.py:48
  266.8 4.1 %collective-permute-start.43 = (bf16[8,104,128]{2,1,0:T(8,128)(2,1)S(1)}, bf16[8,104,128]{2,1,0:T(8,128)(2,1)S(1)}, u32[]{:S(2)}, u32[]{:S(2)}) collective-permute-start(bf16[8,104,128]{2,1,0:T(8,128)(2,1)S(1)} %get-tuple-element.130), channel_id=1, source_target_pairs={{0,1},{1,0},{2,3},{3,2},{4,5},{5,4},{6,7},{7,6},{8,9},{9,8},{10,11... | collective-permute-start | bytes 638984 | tf_op jit(solution)/shard_map/ppermute | solution.py:48
  271.7 3.3 %collective-permute-start.56 = (bf16[16,104,128]{2,1,0:T(8,128)(2,1)S(1)}, bf16[16,104,128]{2,1,0:T(8,128)(2,1)S(1)}, u32[]{:S(2)}, u32[]{:S(2)}) collective-permute-start(bf16[16,104,128]{2,1,0:T(8,128)(2,1)S(1)} %pad_maximum_fusion.20.rest_2_), channel_id=1, source_target_pairs={{0,12},{1,13},{2,14},{3,15},{4,8},{5,9},{6,10},{7,11},{8,4},{9,5},... | collective-permute-start | bytes 1277960 | tf_op jit(solution)/shard_map/ppermute | solution.py:48
  278.1 3.0 collective-permute-done.56.rest_3_
  283.3 5.8 %returns.6.rest_4_ = f32[64,104,128]{2,1,0:T(8,128)S(1)} custom-call(s32[272]{0:T(512)S(1)} %get-tuple-element.79.list_ref, s32[11]{0:T(128)S(1)} %get-tuple-element.153.counts_ref, bf16[16,104,128]{2,1,0:T(8,128)(2,1)S(1)} %pad_maximum_fusion.19.rest_0_, bf16[16,104,128]{2,1,0:T(8,128)(2,1)S(1)} %collective-permute-done.54.rest_1_, ...), custom_call_target="tpu_custom_call" | custom-call | tf_op jit(solution)/shard_map/returns/pallas_call | solution.py:237
  289.1 4.7 %returns.7 = (bf16[32,104,128]{2,1,0:T(8,128)(2,1)S(1)}, f32[32,104,128]{2,1,0:T(8,128)S(1)}) custom-call(s32[272]{0:T(512)S(1)} %get-tuple-element.80.list_ref, s32[11]{0:T(128)S(1)} %get-tuple-element.154.counts_ref, bf16[16,104,128]{2,1,0:T(8,128)(2,1)S(1)} %pad_maximum_fusion.16.rest_0_, bf16[16,104,128]{2,1,0:T(8,128)(2,1)S(1)} %collective-permute-done.42.rest_1_, ...), custom_call_target="tpu_custom_call" | custom-call | tf_op jit(solution)/shard_map/returns/pallas_call | solution.py:260
  296.8 9.1 %collective-permute-done.58 = bf16[16,104,128]{2,1,0:T(8,128)(2,1)S(1)} collective-permute-done((bf16[16,104,128]{2,1,0:T(8,128)(2,1)S(1)}, bf16[16,104,128]{2,1,0:T(8,128)(2,1)S(1)}, u32[]{:S(2)}, u32[]{:S(2)}) %collective-permute-start.58) | collective-permute-done | bytes 426016 | tf_op jit(solution)/shard_map/ppermute | solution.py:48
  307.0 4.9 %collective-permute-done.59 = bf16[8,104,128]{2,1,0:T(8,128)(2,1)S(1)} collective-permute-done((bf16[8,104,128]{2,1,0:T(8,128)(2,1)S(1)}, bf16[8,104,128]{2,1,0:T(8,128)(2,1)S(1)}, u32[]{:S(2)}, u32[]{:S(2)}) %collective-permute-start.59) | collective-permute-done | bytes 213024 | tf_op jit(solution)/shard_map/ppermute | solution.py:48
  (220 shorter events, 110.1 us)
Async XLA Ops:
  7.0 10.7 %collective-permute-start = (bf16[8,104,128]{2,1,0:T(8,128)(2,1)S(1)}, bf16[8,104,128]{2,1,0:T(8,128)(2,1)S(1)}, u32[]{:S(2)}, u32[]{:S(2)}) collective-permute-start(bf16[8,104,128]{2,1,0:T(8,128)(2,1)S(1)} %fusion.47), channel_id=1, source_target_pairs={{0,32},{1,33},{2,34},{3,35},{4,36},{5,37},{6,38},{7,39},{8,40},{9,... | collective-permute-start | bytes 638984 | tf_op jit(solution)/shard_map/ppermute | solution.py:48
  17.7 9.4 %collective-permute-start.1 = (bf16[16,104,128]{2,1,0:T(8,128)(2,1)S(1)}, bf16[16,104,128]{2,1,0:T(8,128)(2,1)S(1)}, u32[]{:S(2)}, u32[]{:S(2)}) collective-permute-start(bf16[16,104,128]{2,1,0:T(8,128)(2,1)S(1)} %pad_maximum_fusion.7), channel_id=1, source_target_pairs={{0,96},{1,97},{2,98},{3,99},{4,100},{5,101},{6,102},{7,103},{8,104... | collective-permute-start | bytes 1277960 | tf_op jit(solution)/shard_map/ppermute | solution.py:48
  28.1 52.8 %all-to-all-start.1 = ((bf16[8,1984,128]{2,1,0:T(8,128)(2,1)}), bf16[8,1984,128]{2,1,0:T(8,128)(2,1)}, u32[]{:S(2)}, u32[]{:S(2)}) async-start(bf16[8,1984,128]{2,1,0:T(8,128)(2,1)} %bitcast.276), calls=%async_computation.1 | async-start | bytes 8126464 | tf_op jit(solution)/shard_map/all_to_all | solution.py:338
  87.8 15.3 %collective-permute-start.15 = (bf16[16,104,128]{2,1,0:T(8,128)(2,1)}, bf16[16,104,128]{2,1,0:T(8,128)(2,1)}, u32[]{:S(2)}, u32[]{:S(2)}) collective-permute-start(bf16[16,104,128]{2,1,0:T(8,128)(2,1)} %get-tuple-element.60), channel_id=1, source_target_pairs={{0,4},{1,5},{2,6},{3,7},{4,0},{5,1},{6,2},{7,3},{8,12},{9,13},{10,... | collective-permute-start | bytes 1277960 | tf_op jit(solution)/shard_map/ppermute | solution.py:48
  89.2 16.4 %collective-permute-start.16 = (bf16[16,104,128]{2,1,0:T(8,128)(2,1)}, bf16[16,104,128]{2,1,0:T(8,128)(2,1)}, u32[]{:S(2)}, u32[]{:S(2)}) collective-permute-start(bf16[16,104,128]{2,1,0:T(8,128)(2,1)} %get-tuple-element.62), channel_id=1, source_target_pairs={{0,12},{1,13},{2,14},{3,15},{4,8},{5,9},{6,10},{7,11},{8,4},{9,5},... | collective-permute-start | bytes 1277960 | tf_op jit(solution)/shard_map/ppermute | solution.py:48
  99.0 11.2 %collective-permute-start.3 = (bf16[16,104,128]{2,1,0:T(8,128)(2,1)S(1)}, bf16[16,104,128]{2,1,0:T(8,128)(2,1)S(1)}, u32[]{:S(2)}, u32[]{:S(2)}) collective-permute-start(bf16[16,104,128]{2,1,0:T(8,128)(2,1)S(1)} %get-tuple-element.56), channel_id=1, source_target_pairs={{0,1},{1,0},{2,3},{3,2},{4,5},{5,4},{6,7},{7,6},{8,9},{9,8},{10,11... | collective-permute-start | bytes 1277960 | tf_op jit(solution)/shard_map/ppermute | solution.py:48
  100.9 12.3 %collective-permute-start.4 = (bf16[16,104,128]{2,1,0:T(8,128)(2,1)S(1)}, bf16[16,104,128]{2,1,0:T(8,128)(2,1)S(1)}, u32[]{:S(2)}, u32[]{:S(2)}) collective-permute-start(bf16[16,104,128]{2,1,0:T(8,128)(2,1)S(1)} %get-tuple-element.58), channel_id=1, source_target_pairs={{0,3},{1,2},{2,1},{3,0},{4,7},{5,6},{6,5},{7,4},{8,11},{9,10},{10,... | collective-permute-start | bytes 1277960 | tf_op jit(solution)/shard_map/ppermute | solution.py:48
  104.2 9.6 %collective-permute-start.17 = (bf16[8,104,128]{2,1,0:T(8,128)(2,1)S(1)}, bf16[8,104,128]{2,1,0:T(8,128)(2,1)S(1)}, u32[]{:S(2)}, u32[]{:S(2)}) collective-permute-start(bf16[8,104,128]{2,1,0:T(8,128)(2,1)S(1)} %get-tuple-element.120), channel_id=1, source_target_pairs={{0,12},{1,13},{2,14},{3,15},{4,8},{5,9},{6,10},{7,11},{8,4},{9,5},... | collective-permute-start | bytes 638984 | tf_op jit(solution)/shard_map/ppermute | solution.py:48
  114.0 8.7 %collective-permute-start.19 = (bf16[2,4,104,128]{3,2,1,0:T(8,128)(2,1)S(1)}, bf16[2,4,104,128]{3,2,1,0:T(8,128)(2,1)S(1)}, u32[]{:S(2)}, u32[]{:S(2)}) collective-permute-start(bf16[2,4,104,128]{3,2,1,0:T(8,128)(2,1)S(1)} %get-tuple-element.116), channel_id=1, source_target_pairs={{0,1},{1,0},{2,3},{3,2},{4,5},{5,4},{6,7},{7,6},{8,9},{9,8},{10,11... | collective-permute-start | bytes 638984 | tf_op jit(solution)/shard_map/ppermute | solution.py:48
  140.4 7.8 %collective-permute-start.10 = (bf16[2,4,104,128]{3,2,1,0:T(8,128)(2,1)S(1)}, bf16[2,4,104,128]{3,2,1,0:T(8,128)(2,1)S(1)}, u32[]{:S(2)}, u32[]{:S(2)}) collective-permute-start(bf16[2,4,104,128]{3,2,1,0:T(8,128)(2,1)S(1)} %pad_maximum_fusion.25), channel_id=1, source_target_pairs={{0,4},{1,5},{2,6},{3,7},{4,0},{5,1},{6,2},{7,3},{8,12},{9,13},{10,... | collective-permute-start | bytes 638984 | tf_op jit(solution)/shard_map/ppermute | solution.py:48
  141.5 11.2 %collective-permute-start.25 = (bf16[8,104,128]{2,1,0:T(8,128)(2,1)S(1)}, bf16[8,104,128]{2,1,0:T(8,128)(2,1)S(1)}, u32[]{:S(2)}, u32[]{:S(2)}) collective-permute-start(bf16[8,104,128]{2,1,0:T(8,128)(2,1)S(1)} %get-tuple-element.132), channel_id=1, source_target_pairs={{0,4},{1,5},{2,6},{3,7},{4,0},{5,1},{6,2},{7,3},{8,12},{9,13},{10,... | collective-permute-start | bytes 638984 | tf_op jit(solution)/shard_map/ppermute | solution.py:48
  142.7 10.7 %collective-permute-start.23 = (bf16[8,104,128]{2,1,0:T(8,128)(2,1)S(1)}, bf16[8,104,128]{2,1,0:T(8,128)(2,1)S(1)}, u32[]{:S(2)}, u32[]{:S(2)}) collective-permute-start(bf16[8,104,128]{2,1,0:T(8,128)(2,1)S(1)} %get-tuple-element.133), channel_id=1, source_target_pairs={{0,12},{1,13},{2,14},{3,15},{4,8},{5,9},{6,10},{7,11},{8,4},{9,5},... | collective-permute-start | bytes 638984 | tf_op jit(solution)/shard_map/ppermute | solution.py:48
  152.8 9.4 %collective-permute-start.26 = (bf16[16,104,128]{2,1,0:T(8,128)(2,1)S(1)}, bf16[16,104,128]{2,1,0:T(8,128)(2,1)S(1)}, u32[]{:S(2)}, u32[]{:S(2)}) collective-permute-start(bf16[16,104,128]{2,1,0:T(8,128)(2,1)S(1)} %pad_maximum_fusion.13.rest_2_), channel_id=1, source_target_pairs={{0,12},{1,13},{2,14},{3,15},{4,8},{5,9},{6,10},{7,11},{8,4},{9,5},... | collective-permute-start | bytes 1277960 | tf_op jit(solution)/shard_map/ppermute | solution.py:48
  153.5 8.7 %collective-permute-start.24 = (bf16[16,104,128]{2,1,0:T(8,128)(2,1)S(1)}, bf16[16,104,128]{2,1,0:T(8,128)(2,1)S(1)}, u32[]{:S(2)}, u32[]{:S(2)}) collective-permute-start(bf16[16,104,128]{2,1,0:T(8,128)(2,1)S(1)} %pad_maximum_fusion.12.rest_0_), channel_id=1, source_target_pairs={{0,4},{1,5},{2,6},{3,7},{4,0},{5,1},{6,2},{7,3},{8,12},{9,13},{10,... | collective-permute-start | bytes 1277960 | tf_op jit(solution)/shard_map/ppermute | solution.py:48
  155.2 12.8 %collective-permute-start.14 = (bf16[16,104,128]{2,1,0:T(8,128)(2,1)S(1)}, bf16[16,104,128]{2,1,0:T(8,128)(2,1)S(1)}, u32[]{:S(2)}, u32[]{:S(2)}) collective-permute-start(bf16[16,104,128]{2,1,0:T(8,128)(2,1)S(1)} %pad_maximum_fusion.10.rest_2_), channel_id=1, source_target_pairs={{0,3},{1,2},{2,1},{3,0},{4,7},{5,6},{6,5},{7,4},{8,11},{9,10},{10,... | collective-permute-start | bytes 1277960 | tf_op jit(solution)/shard_map/ppermute | solution.py:48
  156.1 11.9 %collective-permute-start.12 = (bf16[16,104,128]{2,1,0:T(8,128)(2,1)S(1)}, bf16[16,104,128]{2,1,0:T(8,128)(2,1)S(1)}, u32[]{:S(2)}, u32[]{:S(2)}) collective-permute-start(bf16[16,104,128]{2,1,0:T(8,128)(2,1)S(1)} %pad_maximum_fusion.9.rest_0_), channel_id=1, source_target_pairs={{0,1},{1,0},{2,3},{3,2},{4,5},{5,4},{6,7},{7,6},{8,9},{9,8},{10,11... | collective-permute-start | bytes 1277960 | tf_op jit(solution)/shard_map/ppermute | solution.py:48
  175.4 9.4 %collective-permute-start.28 = (bf16[16,104,128]{2,1,0:T(8,128)(2,1)S(1)}, bf16[16,104,128]{2,1,0:T(8,128)(2,1)S(1)}, u32[]{:S(2)}, u32[]{:S(2)}) collective-permute-start(bf16[16,104,128]{2,1,0:T(8,128)(2,1)S(1)} %slice.691), channel_id=1, source_target_pairs={{0,96},{1,97},{2,98},{3,99},{4,100},{5,101},{6,102},{7,103},{8,104... | collective-permute-start | bytes 1277960 | tf_op jit(solution)/shard_map/ppermute | solution.py:48
  197.0 9.4 %collective-permute-start.31 = (bf16[16,104,128]{2,1,0:T(8,128)(2,1)S(1)}, bf16[16,104,128]{2,1,0:T(8,128)(2,1)S(1)}, u32[]{:S(2)}, u32[]{:S(2)}) collective-permute-start(bf16[16,104,128]{2,1,0:T(8,128)(2,1)S(1)} %pad_maximum_fusion.14), channel_id=1, source_target_pairs={{0,96},{1,97},{2,98},{3,99},{4,100},{5,101},{6,102},{7,103},{8,104... | collective-permute-start | bytes 1277960 | tf_op jit(solution)/shard_map/ppermute | solution.py:48
  215.0 11.4 %collective-permute-start.45 = (bf16[16,104,128]{2,1,0:T(8,128)(2,1)S(1)}, bf16[16,104,128]{2,1,0:T(8,128)(2,1)S(1)}, u32[]{:S(2)}, u32[]{:S(2)}) collective-permute-start(bf16[16,104,128]{2,1,0:T(8,128)(2,1)S(1)} %get-tuple-element.70), channel_id=1, source_target_pairs={{0,4},{1,5},{2,6},{3,7},{4,0},{5,1},{6,2},{7,3},{8,12},{9,13},{10,... | collective-permute-start | bytes 1277960 | tf_op jit(solution)/shard_map/ppermute | solution.py:48
  215.1 13.4 %collective-permute-start.46 = (bf16[16,104,128]{2,1,0:T(8,128)(2,1)S(1)}, bf16[16,104,128]{2,1,0:T(8,128)(2,1)S(1)}, u32[]{:S(2)}, u32[]{:S(2)}) collective-permute-start(bf16[16,104,128]{2,1,0:T(8,128)(2,1)S(1)} %get-tuple-element.72), channel_id=1, source_target_pairs={{0,12},{1,13},{2,14},{3,15},{4,8},{5,9},{6,10},{7,11},{8,4},{9,5},... | collective-permute-start | bytes 1277960 | tf_op jit(solution)/shard_map/ppermute | solution.py:48
  221.3 11.8 %collective-permute-start.33 = (bf16[16,104,128]{2,1,0:T(8,128)(2,1)S(1)}, bf16[16,104,128]{2,1,0:T(8,128)(2,1)S(1)}, u32[]{:S(2)}, u32[]{:S(2)}) collective-permute-start(bf16[16,104,128]{2,1,0:T(8,128)(2,1)S(1)} %get-tuple-element.66), channel_id=1, source_target_pairs={{0,1},{1,0},{2,3},{3,2},{4,5},{5,4},{6,7},{7,6},{8,9},{9,8},{10,11... | collective-permute-start | bytes 1277960 | tf_op jit(solution)/shard_map/ppermute | solution.py:48
  222.5 12.2 %collective-permute-start.34 = (bf16[16,104,128]{2,1,0:T(8,128)(2,1)S(1)}, bf16[16,104,128]{2,1,0:T(8,128)(2,1)S(1)}, u32[]{:S(2)}, u32[]{:S(2)}) collective-permute-start(bf16[16,104,128]{2,1,0:T(8,128)(2,1)S(1)} %get-tuple-element.68), channel_id=1, source_target_pairs={{0,3},{1,2},{2,1},{3,0},{4,7},{5,6},{6,5},{7,4},{8,11},{9,10},{10,... | collective-permute-start | bytes 1277960 | tf_op jit(solution)/shard_map/ppermute | solution.py:48
  226.5 8.6 %collective-permute-start.47 = (bf16[8,104,128]{2,1,0:T(8,128)(2,1)S(1)}, bf16[8,104,128]{2,1,0:T(8,128)(2,1)S(1)}, u32[]{:S(2)}, u32[]{:S(2)}) collective-permute-start(bf16[8,104,128]{2,1,0:T(8,128)(2,1)S(1)} %get-tuple-element.108), channel_id=1, source_target_pairs={{0,12},{1,13},{2,14},{3,15},{4,8},{5,9},{6,10},{7,11},{8,4},{9,5},... | collective-permute-start | bytes 638984 | tf_op jit(solution)/shard_map/ppermute | solution.py:48
  235.1 9.6 %collective-permute-start.49 = (bf16[2,4,104,128]{3,2,1,0:T(8,128)(2,1)S(1)}, bf16[2,4,104,128]{3,2,1,0:T(8,128)(2,1)S(1)}, u32[]{:S(2)}, u32[]{:S(2)}) collective-permute-start(bf16[2,4,104,128]{3,2,1,0:T(8,128)(2,1)S(1)} %get-tuple-element.104), channel_id=1, source_target_pairs={{0,1},{1,0},{2,3},{3,2},{4,5},{5,4},{6,7},{7,6},{8,9},{9,8},{10,11... | collective-permute-start | bytes 638984 | tf_op jit(solution)/shard_map/ppermute | solution.py:48
  263.5 8.2 %collective-permute-start.55 = (bf16[8,104,128]{2,1,0:T(8,128)(2,1)S(1)}, bf16[8,104,128]{2,1,0:T(8,128)(2,1)S(1)}, u32[]{:S(2)}, u32[]{:S(2)}) collective-permute-start(bf16[8,104,128]{2,1,0:T(8,128)(2,1)S(1)} %get-tuple-element.128), channel_id=1, source_target_pairs={{0,4},{1,5},{2,6},{3,7},{4,0},{5,1},{6,2},{7,3},{8,12},{9,13},{10,... | collective-permute-start | bytes 638984 | tf_op jit(solution)/shard_map/ppermute | solution.py:48
  264.1 11.0 %collective-permute-start.53 = (bf16[8,104,128]{2,1,0:T(8,128)(2,1)S(1)}, bf16[8,104,128]{2,1,0:T(8,128)(2,1)S(1)}, u32[]{:S(2)}, u32[]{:S(2)}) collective-permute-start(bf16[8,104,128]{2,1,0:T(8,128)(2,1)S(1)} %get-tuple-element.129), channel_id=1, source_target_pairs={{0,12},{1,13},{2,14},{3,15},{4,8},{5,9},{6,10},{7,11},{8,4},{9,5},... | collective-permute-start | bytes 638984 | tf_op jit(solution)/shard_map/ppermute | solution.py:48
  266.8 10.2 %collective-permute-start.43 = (bf16[8,104,128]{2,1,0:T(8,128)(2,1)S(1)}, bf16[8,104,128]{2,1,0:T(8,128)(2,1)S(1)}, u32[]{:S(2)}, u32[]{:S(2)}) collective-permute-start(bf16[8,104,128]{2,1,0:T(8,128)(2,1)S(1)} %get-tuple-element.130), channel_id=1, source_target_pairs={{0,1},{1,0},{2,3},{3,2},{4,5},{5,4},{6,7},{7,6},{8,9},{9,8},{10,11... | collective-permute-start | bytes 638984 | tf_op jit(solution)/shard_map/ppermute | solution.py:48
  271.7 9.4 %collective-permute-start.56 = (bf16[16,104,128]{2,1,0:T(8,128)(2,1)S(1)}, bf16[16,104,128]{2,1,0:T(8,128)(2,1)S(1)}, u32[]{:S(2)}, u32[]{:S(2)}) collective-permute-start(bf16[16,104,128]{2,1,0:T(8,128)(2,1)S(1)} %pad_maximum_fusion.20.rest_2_), channel_id=1, source_target_pairs={{0,12},{1,13},{2,14},{3,15},{4,8},{5,9},{6,10},{7,11},{8,4},{9,5},... | collective-permute-start | bytes 1277960 | tf_op jit(solution)/shard_map/ppermute | solution.py:48
  275.1 8.2 %collective-permute-start.54 = (bf16[16,104,128]{2,1,0:T(8,128)(2,1)S(1)}, bf16[16,104,128]{2,1,0:T(8,128)(2,1)S(1)}, u32[]{:S(2)}, u32[]{:S(2)}) collective-permute-start(bf16[16,104,128]{2,1,0:T(8,128)(2,1)S(1)} %pad_maximum_fusion.19.rest_0_), channel_id=1, source_target_pairs={{0,4},{1,5},{2,6},{3,7},{4,0},{5,1},{6,2},{7,3},{8,12},{9,13},{10,... | collective-permute-start | bytes 1277960 | tf_op jit(solution)/shard_map/ppermute | solution.py:48
  277.1 12.0 %collective-permute-start.44 = (bf16[16,104,128]{2,1,0:T(8,128)(2,1)S(1)}, bf16[16,104,128]{2,1,0:T(8,128)(2,1)S(1)}, u32[]{:S(2)}, u32[]{:S(2)}) collective-permute-start(bf16[16,104,128]{2,1,0:T(8,128)(2,1)S(1)} %pad_maximum_fusion.17.rest_2_), channel_id=1, source_target_pairs={{0,3},{1,2},{2,1},{3,0},{4,7},{5,6},{6,5},{7,4},{8,11},{9,10},{10,... | collective-permute-start | bytes 1277960 | tf_op jit(solution)/shard_map/ppermute | solution.py:48
  278.0 11.1 %collective-permute-start.42 = (bf16[16,104,128]{2,1,0:T(8,128)(2,1)S(1)}, bf16[16,104,128]{2,1,0:T(8,128)(2,1)S(1)}, u32[]{:S(2)}, u32[]{:S(2)}) collective-permute-start(bf16[16,104,128]{2,1,0:T(8,128)(2,1)S(1)} %pad_maximum_fusion.16.rest_0_), channel_id=1, source_target_pairs={{0,1},{1,0},{2,3},{3,2},{4,5},{5,4},{6,7},{7,6},{8,9},{9,8},{10,11... | collective-permute-start | bytes 1277960 | tf_op jit(solution)/shard_map/ppermute | solution.py:48
  296.5 9.4 %collective-permute-start.58 = (bf16[16,104,128]{2,1,0:T(8,128)(2,1)S(1)}, bf16[16,104,128]{2,1,0:T(8,128)(2,1)S(1)}, u32[]{:S(2)}, u32[]{:S(2)}) collective-permute-start(bf16[16,104,128]{2,1,0:T(8,128)(2,1)S(1)} %slice.690), channel_id=1, source_target_pairs={{0,96},{1,97},{2,98},{3,99},{4,100},{5,101},{6,102},{7,103},{8,104... | collective-permute-start | bytes 1277960 | tf_op jit(solution)/shard_map/ppermute | solution.py:48
  (33 other events, 249.3 us)
